TPU v7x, 32 devices: a whole 2x2x4 slice. The times are simulated.
32 devices in a mesh: rows: 4 (over y, x), cols: 8 (over z, core).
Axes of the slice: x: 2, y: 2, z: 4, core: 2. Of those that a mesh axis runs over, the one named last changes fastest.
Arguments:
- latent1: bfloat16 [64, 512, 320], P('rows', 'cols'), may hold values from -15 to 15, as said below
- norm1a_g: float32 [320], replicated, may hold values from 0.25 to 1.75
- norm1a_b: float32 [320], replicated, may hold values from -3 to 3
- conv1a_w: bfloat16 [3, 3, 320, 320], replicated, may hold values from -0.109375 to 0.109375
- norm1b_g: float32 [320], replicated, may hold values from 0.25 to 1.75
- norm1b_b: float32 [320], replicated, may hold values from -3 to 3
- conv1b_w: bfloat16 [3, 3, 320, 320], replicated, may hold values from -0.109375 to 0.109375
- conv1b_b: float32 [320], replicated, may hold values from -3 to 3
- feat3: bfloat16 [16, 128, 1280], P('rows', 'cols'), may hold values from -15 to 15, as said below
- adapter3: bfloat16 [16, 128, 1280], P('rows', 'cols'), may hold values from -15 to 15, as said below
- norm3a_g: float32 [1280], replicated, may hold values from 0.25 to 1.75
- norm3a_b: float32 [1280], replicated, may hold values from -3 to 3
- conv3a_w: bfloat16 [3, 3, 1280, 1280], P(None, None, None, 'cols'), may hold values from -0.0546875 to 0.0546875
- norm3b_g: float32 [1280], P('cols'), may hold values from 0.25 to 1.75
- norm3b_b: float32 [1280], P('cols'), may hold values from -3 to 3
- conv3b_w: bfloat16 [3, 3, 1280, 1280], P(None, None, None, 'cols'), may hold values from -0.0546875 to 0.0546875
- conv3b_b: float32 [1280], P('cols'), may hold values from -3 to 3
Outputs:
- out1: bfloat16 [64, 512, 320], P('rows', 'cols')
- out3: bfloat16 [16, 128, 1280], P('rows', None, 'cols')
Inputs may be any that keep to these rules, and one draw needn't show every extreme that they name: `latent1`: real values. `feat3`: real values. `adapter3`: real values.
All inputs are finite; a program needn't handle non-finite values.
Results may differ from a plain program's by a relative error of at most 0.0052.
Values may be sent and summed in bfloat16 or wider, within the bound.
No kernel may reach another device: no remote copies, remote signals or barrier semaphores. Data moves between devices by JAX's collectives and lax.ppermute only.
A program may use at most 128 MiB of HBM per device.

v0:
```python
import jax
import jax.numpy as jnp
from jax import lax
from jax.sharding import PartitionSpec as P

C1 = 320
C3 = 1280


norm_eps = 1e-05


def extended(block, sides, width):
    for axis, dim in sides:
        count = lax.axis_size(axis)
        forward = [(i, i + 1) for i in range(count - 1)]
        backward = [(target, source) for source, target in forward]
        low = lax.ppermute(
            lax.slice_in_dim(block, block.shape[dim] - width, None, axis=dim), axis, forward
        )
        high = lax.ppermute(lax.slice_in_dim(block, 0, width, axis=dim), axis, backward)
        block = jnp.concatenate([low, block, high], axis=dim)
    return block


def conv_valid(padded, kernel):
    return lax.conv_general_dilated(
        padded[None],
        kernel,
        (1, 1),
        "VALID",
        dimension_numbers=("NHWC", "HWIO", "NHWC"),
        preferred_element_type=jnp.float32,
    )[0]


def moments(value, group_width):
    height, width, chans = value.shape
    grouped = value.astype(jnp.float32).reshape(height, width, chans // group_width, group_width)
    return (jnp.sum(grouped, axis=(0, 1, 3)), jnp.sum(grouped * grouped, axis=(0, 1, 3)))


def normalize(value, sums, squares, count, gain, shift):
    height, width, chans = value.shape
    groups = sums.shape[0]
    mean = sums / count
    inverse = lax.rsqrt(squares / count - mean * mean + norm_eps)
    grouped = value.astype(jnp.float32).reshape(height, width, groups, chans // groups)
    normed = ((grouped - mean[:, None]) * inverse[:, None]).reshape(height, width, chans)
    return jax.nn.silu(normed * gain + shift).astype(jnp.bfloat16)


def level3_totals(values, group_width):
    sums, squares = moments(values, group_width)
    return lax.psum((sums, squares), "rows")


def folder(kernel, total, piece):
    height = total.shape[0]
    width = total.shape[1]
    count = piece.shape[2]
    wide = jnp.pad(piece, ((0, 0), (1, 1), (0, 0)))
    taps = [wide[dy : dy + height, dx : dx + width, :] for dy in range(3) for dx in range(3)]
    patches = jnp.concatenate(taps, axis=2).reshape(height * width, 9 * count)
    weights = kernel.reshape(9 * count, kernel.shape[3])
    product = jnp.dot(patches, weights, preferred_element_type=jnp.float32)
    return product.reshape(height, width, kernel.shape[3])


def body(
    latent1,
    norm1a_g,
    norm1a_b,
    conv1a_w,
    norm1b_g,
    norm1b_b,
    conv1b_w,
    conv1b_b,
    feat3,
    adapter3,
    norm3a_g,
    norm3a_b,
    conv3a_w,
    norm3b_g,
    norm3b_b,
    conv3b_w,
    conv3b_b,
):
    rows_one = latent1.shape[0]
    cols_one = latent1.shape[1]
    width_one = C1 // 32
    count_one = rows_one * cols_one * lax.axis_size("rows") * lax.axis_size("cols") * width_one
    sums, squares = moments(latent1, width_one)
    sums, squares = lax.psum((sums, squares), ("rows", "cols"))
    act1 = normalize(latent1, sums, squares, count_one, norm1a_g, norm1a_b)
    padded = extended(act1, (("rows", 0), ("cols", 1)), 1)
    hid1 = conv_valid(padded, conv1a_w)
    sums_two, squares_two = moments(hid1, width_one)
    sums_two, squares_two = lax.psum((sums_two, squares_two), ("rows", "cols"))
    act2 = normalize(hid1, sums_two, squares_two, count_one, norm1b_g, norm1b_b)
    padded_two = extended(act2, (("rows", 0), ("cols", 1)), 1)
    out1 = (latent1.astype(jnp.float32) + conv_valid(padded_two, conv1b_w) + conv1b_b).astype(
        jnp.bfloat16
    )
    joined = (feat3.astype(jnp.float32) + adapter3.astype(jnp.float32)).astype(jnp.bfloat16)
    shard = conv3a_w.shape[3]
    height = feat3.shape[0]
    width = feat3.shape[1] * lax.axis_size("cols")
    width_three = C3 // 32
    count_three = height * width * lax.axis_size("rows") * width_three
    empty = jnp.zeros((height, width, shard), jnp.float32)
    edged_tile = extended(joined, (("rows", 0),), 1)
    whole = lax.all_gather(edged_tile, "cols", axis=1, tiled=True)
    local = lax.dynamic_slice_in_dim(whole[1:-1], lax.axis_index("cols") * shard, shard, 2)
    sums_three, squares_three = level3_totals(whole[1:-1], width_three)
    line_ids = lax.axis_index("rows") * height - 1 + jnp.arange(height + 2, dtype=jnp.int32)
    line_ok = (line_ids >= 0) & (line_ids < height * lax.axis_size("rows"))
    act_whole = normalize(whole, sums_three, squares_three, count_three, norm3a_g, norm3a_b)
    act_whole = jnp.where(line_ok[:, None, None], act_whole, jnp.zeros((), jnp.bfloat16))
    hid3 = conv_valid(jnp.pad(act_whole, ((0, 0), (1, 1), (0, 0))), conv3a_w)
    sums_four, squares_four = moments(hid3, width_three)
    sums_four, squares_four = lax.psum((sums_four, squares_four), "rows")
    act4 = normalize(hid3, sums_four, squares_four, count_three, norm3b_g, norm3b_b)
    edged_two = extended(act4, (("rows", 0),), 1)
    second = folder(conv3b_w, empty, lax.all_gather(edged_two, "cols", axis=2, tiled=True))
    out3 = (local.astype(jnp.float32) + second + conv3b_b).astype(jnp.bfloat16)
    return (out1, out3)


def solution(mesh):
    placed = (
        P("rows", "cols", None),
        P(),
        P(),
        P(),
        P(),
        P(),
        P(),
        P(),
        P("rows", "cols", None),
        P("rows", "cols", None),
        P(),
        P(),
        P(None, None, None, "cols"),
        P("cols"),
        P("cols"),
        P(None, None, None, "cols"),
        P("cols"),
    )
    return jax.shard_map(
        body,
        mesh=mesh,
        in_specs=placed,
        out_specs=(P("rows", "cols", None), P("rows", None, "cols")),
        check_vma=False,
    )
```

profile of v0, /device:TPU:4, one launch (start us, length us, event | category | flops | bytes accessed | tf_op | source)
XLA Modules:
  0.0 267.6 jit_solution(1989159942951387046)
XLA Ops:
  7.2 1.2 add_convert_fusion
  8.4 3.4 %collective-permute-start.8 = (bf16[1,16,1280]{2,1,0:T(8,128)(2,1)S(1)}, bf16[1,16,1280]{2,1,0:T(8,128)(2,1)S(1)}, u32[]{:S(2)}, u32[]{:S(2)}) collective-permute-start(bf16[1,16,1280]{2,1,0:T(8,128)(2,1)S(1)} %get-tuple-element.38), channel_id=1, source_target_pairs={{0,8},{8,16},{16,24},{1,9},{9,17},{17,25},{2,10},{10,18},{18,26},{... | collective-permute-start | bytes 122888 | tf_op jit(solution)/shard_map/ppermute | solution.py:18
  11.8 3.3 %collective-permute-start.9 = (bf16[1,16,1280]{2,1,0:T(8,128)(2,1)S(1)}, bf16[1,16,1280]{2,1,0:T(8,128)(2,1)S(1)}, u32[]{:S(2)}, u32[]{:S(2)}) collective-permute-start(bf16[1,16,1280]{2,1,0:T(8,128)(2,1)S(1)} %get-tuple-element.39), channel_id=1, source_target_pairs={{8,0},{16,8},{24,16},{9,1},{17,9},{25,17},{10,2},{18,10},{26,18},{... | collective-permute-start | bytes 122888 | tf_op jit(solution)/shard_map/ppermute | solution.py:21
  15.2 2.5 collective-permute-done.9
  17.7 0.7 pad_maximum_fusion
  18.5 1.6 convert_reduce_fusion.1
  20.4 0.6 reduce_sum.100
  21.0 0.7 reduce_sum.97
  21.7 26.1 %all-gather.3.cloned.1.call-done = bf16[6,128,1280]{2,1,0:T(8,128)(2,1)} async-done(((bf16[6,16,1280]{2,1,0:T(8,128)(2,1)}), bf16[6,128,1280]{2,1,0:T(8,128)(2,1)}) %all-gather.3.cloned.1.call-update) | async-done | bytes 1966096 | tf_op jit(solution)/shard_map/all_gather | solution.py:113
  47.8 1.3 slice-done
  49.2 1.4 copy.113
  50.6 1.8 convert_reduce_fusion
  52.8 8.9 %all-reduce.5 = (f32[32]{0:T(128)S(1)}, f32[32]{0:T(128)S(1)}) all-reduce(f32[32]{0:T(128)S(1)} %reduce_sum.145, f32[32]{0:T(128)S(1)} %reduce_sum.115), channel_id=1, replica_groups=mesh['rows'=4,'cols'=8] {'rows'}, use_global_device_ids=true, to_apply=%region_17.18 | all-reduce | flops 64 | bytes 512 | tf_op jit(solution)/shard_map/psum | solution.py:55
  62.0 3.0 %fusion.11 = bf16[6,128,1280]{2,1,0:T(8,128)(2,1)S(1)} fusion(bf16[6,128,1280]{2,1,0:T(8,128)(2,1)} %all-gather.3.cloned.1.call-done, f32[1280]{0:T(1024)S(1)} %copy-done.4, f32[1280]{0:T(1024)S(1)} %copy-done.5, f32[1280]{0:T(1024)S(1)} %mul.156, f32[1280]{0:T(1024)S(1)} %sub.79, pred[6]{0:T(512)(128)(4,1)S(1)} %compare_and_fusion), kind=kLoop, calls=%fused_computation.20 | loop fusion | flops 10813440 | bytes 3952646 | tf_op jit(solution)/shard_map/jit(_where)/select_n | solution.py:119
  65.1 0.5 pad_bitcast_fusion
  65.5 1.5 pad.13
  67.0 4.2 %reshape.81 = bf16[6,1,8,17,1280]{4,3,2,0,1:T(8,128)(2,1)} reshape(bf16[6,1,136,1280]{3,2,0,1:T(8,128)(2,1)} %pad.13) | data formatting | bytes 4177920 | tf_op jit(solution)/shard_map/conv_general_dilated | solution.py:27
  71.2 2.4 copy.104
  73.6 0.5 copy-done.15
  74.1 3.5 %select_reduce_fusion.3 = (f32[160]{0:T(256)S(1)}, f32[160]{0:T(256)S(1)}, f32[4,8,17,160]{3,1,2,0:T(8,128)S(1)}) fusion(pred[8,17]{0,1:T(8,128)(4,1)S(1)} %copy-done.18, bf16[3,3,1280,160]{2,3,1,0:T(8,128)(2,1)S(1)} %copy-done.15, bf16[6,1,7,2,1280]{4,2,3,0,1:T(8,128)(2,1)S(1)} %slice.109, bf16[6,1,8,17,1280]{4,2,3,0,1:T(8,128)(2,1)S(1)} %copy.104), kind=kOutput, calls=%fused_computation.73 | convolution fusion | flops 2012927744 | bytes 6339976 | tf_op jit(solution)/shard_map/conv_general_dilated | solution.py:27
  78.0 41.2 %all-reduce.3 = (f32[32]{0:T(128)}, f32[32]{0:T(128)}) all-reduce(f32[32]{0:T(128)S(1)} %copy-done.11, f32[32]{0:T(128)S(1)} %copy-done.12), channel_id=1, replica_groups=mesh['rows'=4,'cols'=8] {'rows','cols'}, use_global_device_ids=true, to_apply=%region_5.6 | all-reduce | flops 64 | bytes 512 | tf_op jit(solution)/shard_map/psum | solution.py:94
  119.2 8.7 %all-reduce.4 = (f32[4]{0:T(128)S(1)}, f32[4]{0:T(128)S(1)}) all-reduce(f32[4]{0:T(128)S(1)} %reduce_sum.151, f32[4]{0:T(128)S(1)} %reduce_sum.148), channel_id=1, replica_groups=mesh['rows'=4,'cols'=8] {'rows'}, use_global_device_ids=true, to_apply=%region_23.24 | all-reduce | flops 8 | bytes 64 | tf_op jit(solution)/shard_map/psum | solution.py:122
  128.0 0.7 mul.165
  128.7 0.7 sub.84
  129.7 0.9 copy.114
  130.6 1.2 multiply_convert_fusion.2
  131.9 2.6 collective-permute-start.10
  134.5 4.1 %collective-permute-start.11 = (bf16[1,128,160]{1,2,0:T(8,128)(2,1)S(1)}, bf16[1,128,160]{1,2,0:T(8,128)(2,1)S(1)}, u32[]{:S(2)}, u32[]{:S(2)}) collective-permute-start(bf16[1,128,160]{1,2,0:T(8,128)(2,1)S(1)} %get-tuple-element.37), channel_id=1, source_target_pairs={{8,0},{16,8},{24,16},{9,1},{17,9},{25,17},{10,2},{18,10},{26,18},{... | collective-permute-start | bytes 122888 | tf_op jit(solution)/shard_map/ppermute | solution.py:21
  139.0 1.5 collective-permute-done.11
  140.5 0.7 pad_maximum_fusion.1
  141.3 0.8 fusion.20
  142.3 1.9 collective-permute-start
  144.2 5.3 %collective-permute-start.1 = (bf16[1,64,320]{2,0,1:T(2,128)(2,1)S(1)}, bf16[1,64,320]{2,0,1:T(2,128)(2,1)S(1)}, u32[]{:S(2)}, u32[]{:S(2)}) collective-permute-start(bf16[1,64,320]{2,0,1:T(2,128)(2,1)S(1)} %get-tuple-element.35), channel_id=1, source_target_pairs={{8,0},{16,8},{24,16},{9,1},{17,9},{25,17},{10,2},{18,10},{26,18},{... | collective-permute-start | bytes 122888 | tf_op jit(solution)/shard_map/ppermute | solution.py:21
  149.5 0.7 collective-permute-done
  150.1 1.5 collective-permute-done.1
  151.7 1.3 collective-permute-start.2
  153.0 1.5 collective-permute-start.3
  154.5 2.4 collective-permute-done.3
  156.9 0.7 maximum_bitcast_fusion
  158.3 5.1 %select_reduce_fusion.1 = (f32[320]{0:T(512)S(1)}, f32[320]{0:T(512)S(1)}, f32[16,8,9,320]{3,1,2,0:T(8,128)}) fusion(pred[8,9]{0,1:T(8,128)(4,1)S(1)} %copy-done.19, bf16[3,3,320,320]{3,2,1,0:T(8,128)(2,1)S(1)} %copy-done, bf16[18,1,7,2,320]{4,2,3,0,1:T(8,128)(2,1)S(1)} %slice.100, bf16[18,1,8,9,320]{4,2,3,0,1:T(8,128)(2,1)S(1)} %copy.97), kind=kOutput, calls=%fused_computation.22 | convolution fusion | flops 2128619008 | bytes 4311112 | tf_op jit(solution)/shard_map/conv_general_dilated | solution.py:27
  163.9 44.7 %all-reduce.2 = (f32[32]{0:T(128)S(1)}, f32[32]{0:T(128)S(1)}) all-reduce(f32[32]{0:T(128)S(1)} %reduce_sum.112, f32[32]{0:T(128)S(1)} %reduce_sum.106), channel_id=1, replica_groups=mesh['rows'=4,'cols'=8] {'rows','cols'}, use_global_device_ids=true, to_apply=%region_11.12 | all-reduce | flops 64 | bytes 512 | tf_op jit(solution)/shard_map/psum | solution.py:99
  209.0 1.8 copy.98
  210.8 0.5 multiply_convert_fusion.1
  211.5 2.7 %collective-permute-start.4 = (bf16[1,64,320]{2,0,1:T(2,128)(2,1)S(1)}, bf16[1,64,320]{2,0,1:T(2,128)(2,1)S(1)}, u32[]{:S(2)}, u32[]{:S(2)}) collective-permute-start(bf16[1,64,320]{2,0,1:T(2,128)(2,1)S(1)} %get-tuple-element.32), channel_id=1, source_target_pairs={{0,8},{8,16},{16,24},{1,9},{9,17},{17,25},{2,10},{10,18},{18,26},{... | collective-permute-start | bytes 122888 | tf_op jit(solution)/shard_map/ppermute | solution.py:18
  214.2 4.1 %collective-permute-start.5 = (bf16[1,64,320]{2,0,1:T(2,128)(2,1)S(1)}, bf16[1,64,320]{2,0,1:T(2,128)(2,1)S(1)}, u32[]{:S(2)}, u32[]{:S(2)}) collective-permute-start(bf16[1,64,320]{2,0,1:T(2,128)(2,1)S(1)} %get-tuple-element.33), channel_id=1, source_target_pairs={{8,0},{16,8},{24,16},{9,1},{17,9},{25,17},{10,2},{18,10},{26,18},{... | collective-permute-start | bytes 122888 | tf_op jit(solution)/shard_map/ppermute | solution.py:21
  218.2 1.3 collective-permute-done.4
  219.5 1.2 collective-permute-done.5
  220.7 1.3 collective-permute-start.6
  222.0 1.3 collective-permute-start.7
  223.3 7.4 %copy.111 = bf16[3,3,1280,160]{2,1,0,3:T(4,128)(2,1)} copy(bf16[3,3,1280,160]{2,3,1,0:T(8,128)(2,1)} %param.32) | data formatting | bytes 7372800 | tf_op args[15]
  230.7 9.4 %reshape.109 = bf16[11520,160,1]{0,1,2:T(8,128)(2,1)} reshape(bf16[3,3,1280,160]{2,1,0,3:T(4,128)(2,1)} %copy.111) | data formatting | bytes 7372800 | tf_op jit(solution)/shard_map/reshape | solution.py:65
  240.1 0.7 maximum_bitcast_fusion.1
  241.2 1.2 copy-done.16
  242.5 3.8 %convolution_select_fusion = f32[16,8,9,320]{3,1,2,0:T(8,128)S(1)} fusion(bf16[3,3,320,320]{3,2,1,0:T(8,128)(2,1)S(1)} %copy-done.16, bf16[18,1,7,2,320]{4,2,3,0,1:T(8,128)(2,1)S(1)} %slice.104, bf16[18,1,8,9,320]{4,2,3,0,1:T(8,128)(2,1)S(1)} %copy.100, pred[8,9]{0,1:T(8,128)(4,1)S(1)} %copy-done.19), kind=kOutput, calls=%fused_computation.42 | convolution fusion | flops 2126776320 | bytes 4308552 | tf_op jit(solution)/shard_map/conv_general_dilated | solution.py:27
  246.3 0.3 copy.101
  246.7 0.3 copy-done.10
  247.0 0.5 fusion.23
  247.5 1.1 copy.112
  248.6 2.7 copy.107
  251.7 0.3 slice_dynamic-update-slice_fusion.7
  252.4 0.3 slice_dynamic-update-slice_fusion.5
  253.1 0.3 slice_dynamic-update-slice_fusion.3
  253.4 1.6 copy-done.3
  255.1 5.7 %fusion.45 = bf16[4,128,160]{1,2,0:T(8,128)(2,1)} fusion(bf16[4,128,11520]{2,1,0:T(8,128)(2,1)S(1)} %slice_dynamic-update-slice_fusion.3, bf16[11520,160,1]{0,1,2:T(8,128)(2,1)S(1)} %copy-done.3, f32[160]{0:T(256)S(1)} %copy-done.17, bf16[4,128,1280]{1,2,0:T(8,128)(2,1)} %copy.113, s32[]{:T(128)S(6)} %select_n.7), kind=kOutput, calls=%fused_computation.69 | convolution fusion | flops 1887764480 | bytes 15811204 | tf_op jit(solution)/shard_map/dot_general | solution.py:66
  (101 shorter events, 5.7 us)
Async XLA Ops:
  7.2 150.8 %copy-start = (bf16[3,3,320,320]{3,2,1,0:T(8,128)(2,1)S(1)}, bf16[3,3,320,320]{3,2,1,0:T(8,128)(2,1)}, u32[]{:S(2)}) copy-start(bf16[3,3,320,320]{3,2,1,0:T(8,128)(2,1)} %param.20) | copy-start | bytes 5529604
  7.2 40.7 %all-gather.3.cloned.1.call-start = ((), (), s32[]{:S(2)}) async-start(), calls=%async_computation | async-start | bytes 2211840 | tf_op jit(solution)/shard_map/all_gather | solution.py:113
  8.4 6.8 %collective-permute-start.8 = (bf16[1,16,1280]{2,1,0:T(8,128)(2,1)S(1)}, bf16[1,16,1280]{2,1,0:T(8,128)(2,1)S(1)}, u32[]{:S(2)}, u32[]{:S(2)}) collective-permute-start(bf16[1,16,1280]{2,1,0:T(8,128)(2,1)S(1)} %get-tuple-element.38), channel_id=1, source_target_pairs={{0,8},{8,16},{16,24},{1,9},{9,17},{17,25},{2,10},{10,18},{18,26},{... | collective-permute-start | bytes 122888 | tf_op jit(solution)/shard_map/ppermute | solution.py:18
  11.8 5.9 %collective-permute-start.9 = (bf16[1,16,1280]{2,1,0:T(8,128)(2,1)S(1)}, bf16[1,16,1280]{2,1,0:T(8,128)(2,1)S(1)}, u32[]{:S(2)}, u32[]{:S(2)}) collective-permute-start(bf16[1,16,1280]{2,1,0:T(8,128)(2,1)S(1)} %get-tuple-element.39), channel_id=1, source_target_pairs={{8,0},{16,8},{24,16},{9,1},{17,9},{25,17},{10,2},{18,10},{26,18},{... | collective-permute-start | bytes 122888 | tf_op jit(solution)/shard_map/ppermute | solution.py:21
  18.5 230.1 %all-gather.5.cloned.1.call-start = ((), (), s32[]{:S(2)}) async-start(), calls=%async_computation.1 | async-start | bytes 2211840 | tf_op jit(solution)/shard_map/all_gather | solution.py:125
  47.8 1.3 slice-start
  49.2 12.9 %copy-start.4 = (f32[1280]{0:T(1024)S(1)}, f32[1280]{0:T(1024)}, u32[]{:S(2)}) copy-start(f32[1280]{0:T(1024)} %param.28) | copy-start | bytes 15364
  49.2 12.9 %copy-start.5 = (f32[1280]{0:T(1024)S(1)}, f32[1280]{0:T(1024)}, u32[]{:S(2)}) copy-start(f32[1280]{0:T(1024)} %param.27) | copy-start | bytes 15364
  71.2 2.9 %copy-start.15 = (bf16[3,3,1280,160]{2,3,1,0:T(8,128)(2,1)S(1)}, bf16[3,3,1280,160]{2,3,1,0:T(8,128)(2,1)}, u32[]{:S(2)}) copy-start(bf16[3,3,1280,160]{2,3,1,0:T(8,128)(2,1)} %param.29) | copy-start | bytes 11059204
  71.2 2.9 %copy-start.18 = (pred[8,17]{0,1:T(8,128)(4,1)S(1)}, pred[8,17]{0,1:T(8,128)(4,1)}, u32[]{:S(2)}) copy-start(pred[8,17]{0,1:T(8,128)(4,1)} %constant.75) | copy-start | bytes 412
  74.1 3.9 %copy-start.11 = (f32[32]{0:T(128)S(1)}, f32[32]{0:T(128)}, u32[]{:S(2)}) copy-start(f32[32]{0:T(128)} %reduce_sum.100) | copy-start | bytes 388
  74.1 3.9 %copy-start.12 = (f32[32]{0:T(128)S(1)}, f32[32]{0:T(128)}, u32[]{:S(2)}) copy-start(f32[32]{0:T(128)} %reduce_sum.97) | copy-start | bytes 388
  129.4 11.9 %copy-start.2 = (bf16[16,64,320]{2,1,0:T(8,128)(2,1)S(1)}, bf16[16,64,320]{2,1,0:T(8,128)(2,1)}, u32[]{:S(2)}) copy-start(bf16[16,64,320]{2,1,0:T(8,128)(2,1)} %param.17) | copy-start | bytes 1966084
  129.6 9.0 %copy-start.13 = (f32[32]{0:T(128)S(1)}, f32[32]{0:T(128)}, u32[]{:S(2)}) copy-start(f32[32]{0:T(128)} %get-tuple-element.22) | copy-start | bytes 388
  129.6 9.0 %copy-start.14 = (f32[32]{0:T(128)S(1)}, f32[32]{0:T(128)}, u32[]{:S(2)}) copy-start(f32[32]{0:T(128)} %get-tuple-element.23) | copy-start | bytes 388
  129.6 11.7 %copy-start.6 = (f32[320]{0:T(512)S(1)}, f32[320]{0:T(512)}, u32[]{:S(2)}) copy-start(f32[320]{0:T(512)} %param.19) | copy-start | bytes 3844
  129.6 11.7 %copy-start.7 = (f32[320]{0:T(512)S(1)}, f32[320]{0:T(512)}, u32[]{:S(2)}) copy-start(f32[320]{0:T(512)} %param.18) | copy-start | bytes 3844
  131.9 7.2 %collective-permute-start.10 = (bf16[1,128,160]{1,2,0:T(8,128)(2,1)S(1)}, bf16[1,128,160]{1,2,0:T(8,128)(2,1)S(1)}, u32[]{:S(2)}, u32[]{:S(2)}) collective-permute-start(bf16[1,128,160]{1,2,0:T(8,128)(2,1)S(1)} %get-tuple-element.36), channel_id=1, source_target_pairs={{0,8},{8,16},{16,24},{1,9},{9,17},{17,25},{2,10},{10,18},{18,26},{... | collective-permute-start | bytes 122888 | tf_op jit(solution)/shard_map/ppermute | solution.py:18
  134.5 6.0 %collective-permute-start.11 = (bf16[1,128,160]{1,2,0:T(8,128)(2,1)S(1)}, bf16[1,128,160]{1,2,0:T(8,128)(2,1)S(1)}, u32[]{:S(2)}, u32[]{:S(2)}) collective-permute-start(bf16[1,128,160]{1,2,0:T(8,128)(2,1)S(1)} %get-tuple-element.37), channel_id=1, source_target_pairs={{8,0},{16,8},{24,16},{9,1},{17,9},{25,17},{10,2},{18,10},{26,18},{... | collective-permute-start | bytes 122888 | tf_op jit(solution)/shard_map/ppermute | solution.py:21
  142.3 7.9 %collective-permute-start = (bf16[1,64,320]{2,0,1:T(2,128)(2,1)S(1)}, bf16[1,64,320]{2,0,1:T(2,128)(2,1)S(1)}, u32[]{:S(2)}, u32[]{:S(2)}) collective-permute-start(bf16[1,64,320]{2,0,1:T(2,128)(2,1)S(1)} %get-tuple-element.34), channel_id=1, source_target_pairs={{0,8},{8,16},{16,24},{1,9},{9,17},{17,25},{2,10},{10,18},{18,26},{... | collective-permute-start | bytes 122888 | tf_op jit(solution)/shard_map/ppermute | solution.py:18
  144.2 7.5 %collective-permute-start.1 = (bf16[1,64,320]{2,0,1:T(2,128)(2,1)S(1)}, bf16[1,64,320]{2,0,1:T(2,128)(2,1)S(1)}, u32[]{:S(2)}, u32[]{:S(2)}) collective-permute-start(bf16[1,64,320]{2,0,1:T(2,128)(2,1)S(1)} %get-tuple-element.35), channel_id=1, source_target_pairs={{8,0},{16,8},{24,16},{9,1},{17,9},{25,17},{10,2},{18,10},{26,18},{... | collective-permute-start | bytes 122888 | tf_op jit(solution)/shard_map/ppermute | solution.py:21
  151.7 2.8 %collective-permute-start.2 = (bf16[18,1,320]{2,0,1:T(8,128)(2,1)S(1)}, bf16[18,1,320]{2,0,1:T(8,128)(2,1)S(1)}, u32[]{:S(2)}, u32[]{:S(2)}) collective-permute-start(bf16[18,1,320]{2,0,1:T(8,128)(2,1)S(1)} %get-tuple-element.30), channel_id=1, source_target_pairs={{0,1},{1,2},{2,3},{3,4},{4,5},{5,6},{6,7},{8,9},{9,10},{10,11},{11... | collective-permute-start | bytes 34568 | tf_op jit(solution)/shard_map/ppermute | solution.py:18
  153.0 3.9 %collective-permute-start.3 = (bf16[18,1,320]{2,0,1:T(8,128)(2,1)S(1)}, bf16[18,1,320]{2,0,1:T(8,128)(2,1)S(1)}, u32[]{:S(2)}, u32[]{:S(2)}) collective-permute-start(bf16[18,1,320]{2,0,1:T(8,128)(2,1)S(1)} %get-tuple-element.31), channel_id=1, source_target_pairs={{1,0},{2,1},{3,2},{4,3},{5,4},{6,5},{7,6},{9,8},{10,9},{11,10},{12... | collective-permute-start | bytes 34568 | tf_op jit(solution)/shard_map/ppermute | solution.py:21
  157.6 0.7 copy-start.19
  163.4 47.3 %copy-start.8 = (f32[320]{0:T(512)S(1)}, f32[320]{0:T(512)}, u32[]{:S(2)}) copy-start(f32[320]{0:T(512)} %param.22) | copy-start | bytes 3844
  163.4 47.4 %copy-start.9 = (f32[320]{0:T(512)S(1)}, f32[320]{0:T(512)}, u32[]{:S(2)}) copy-start(f32[320]{0:T(512)} %param.21) | copy-start | bytes 3844
  211.5 8.0 %collective-permute-start.4 = (bf16[1,64,320]{2,0,1:T(2,128)(2,1)S(1)}, bf16[1,64,320]{2,0,1:T(2,128)(2,1)S(1)}, u32[]{:S(2)}, u32[]{:S(2)}) collective-permute-start(bf16[1,64,320]{2,0,1:T(2,128)(2,1)S(1)} %get-tuple-element.32), channel_id=1, source_target_pairs={{0,8},{8,16},{16,24},{1,9},{9,17},{17,25},{2,10},{10,18},{18,26},{... | collective-permute-start | bytes 122888 | tf_op jit(solution)/shard_map/ppermute | solution.py:18
  214.2 6.5 %collective-permute-start.5 = (bf16[1,64,320]{2,0,1:T(2,128)(2,1)S(1)}, bf16[1,64,320]{2,0,1:T(2,128)(2,1)S(1)}, u32[]{:S(2)}, u32[]{:S(2)}) collective-permute-start(bf16[1,64,320]{2,0,1:T(2,128)(2,1)S(1)} %get-tuple-element.33), channel_id=1, source_target_pairs={{8,0},{16,8},{24,16},{9,1},{17,9},{25,17},{10,2},{18,10},{26,18},{... | collective-permute-start | bytes 122888 | tf_op jit(solution)/shard_map/ppermute | solution.py:21
  220.7 19.4 %collective-permute-start.6 = (bf16[18,1,320]{2,0,1:T(8,128)(2,1)S(1)}, bf16[18,1,320]{2,0,1:T(8,128)(2,1)S(1)}, u32[]{:S(2)}, u32[]{:S(2)}) collective-permute-start(bf16[18,1,320]{2,0,1:T(8,128)(2,1)S(1)} %get-tuple-element.28), channel_id=1, source_target_pairs={{0,1},{1,2},{2,3},{3,4},{4,5},{5,6},{6,7},{8,9},{9,10},{10,11},{11... | collective-permute-start | bytes 34568 | tf_op jit(solution)/shard_map/ppermute | solution.py:18
  222.0 18.1 %collective-permute-start.7 = (bf16[18,1,320]{2,0,1:T(8,128)(2,1)S(1)}, bf16[18,1,320]{2,0,1:T(8,128)(2,1)S(1)}, u32[]{:S(2)}, u32[]{:S(2)}) collective-permute-start(bf16[18,1,320]{2,0,1:T(8,128)(2,1)S(1)} %get-tuple-element.29), channel_id=1, source_target_pairs={{1,0},{2,1},{3,2},{4,3},{5,4},{6,5},{7,6},{9,8},{10,9},{11,10},{12... | collective-permute-start | bytes 34568 | tf_op jit(solution)/shard_map/ppermute | solution.py:21
  240.9 1.6 copy-start.16
  246.3 0.7 copy-start.10
  253.0 2.0 copy-start.3
  253.1 1.9 copy-start.17
  255.1 5.7 %copy-start.1 = (bf16[3,3,320,320]{3,2,1,0:T(8,128)(2,1)S(1)}, bf16[3,3,320,320]{3,2,1,0:T(8,128)(2,1)}, u32[]{:S(2)}) copy-start(bf16[3,3,320,320]{3,2,1,0:T(8,128)(2,1)} %param.20) | copy-start | bytes 5529604
Sparse Core Ops, SparseCore 0:
  18.6 29.1 all-gather.2
  141.4 28.6 all-gather.4
where the time goes:
time: 273 us; the launch traced here: 268 us
  blocking collectives  103 us (38%)
  local copies, waits for them, and re-layouts  45.5 us (17%)
  waiting for transfers between devices  37.3 us (14%)
  starting transfers between devices  32.9 us (12%)
  matrix products  18.1 us (7%)
  other arithmetic  15.6 us (6%)
  between operations  14.7 us (5%)
    psum x1, blocking collectives, body(): sums_two, squares_two = lax.psum((sums_two, squares_two), ('rows', 'cols'))  44.7 us
    psum x1, blocking collectives, body(): sums, squares = lax.psum((sums, squares), ('rows', 'cols'))  41.2 us
    all_gather x1, waiting for transfers between devices, body(): whole = lax.all_gather(edged_tile, 'cols', axis=1, tiled=True)  26.1 us
    ppermute x6, starting transfers between devices, extended(): lax.ppermute(lax.slice_in_dim(block, 0, width, axis=dim), axis, backward)  19.6 us
    unnamed x52, local copies, waits for them, and re-layouts  16.6 us
    ppermute x6, starting transfers between devices, extended(): lax.ppermute(lax.slice_in_dim(block, block.shape[dim] - width, None, axis...  13.2 us
    conv_general_dilated x3, matrix products, conv_valid(): lax.conv_general_dilated(padded[None], kernel, (1, 1), 'VALID', dimension...  12.5 us
    conv_general_dilated x11, local copies, waits for them, and re-layouts, conv_valid(): lax.conv_general_dilated(padded[None], kernel, (1, 1), 'VALID', dimension...  9.39 us
  transfers between devices with their start and end apart: 14, of which 8 were waited for; matrix products, arithmetic and copies ran while one was open for 14% of the time, Pallas kernels for 0%

commit v1 on v0

--- a/solution.py
+++ b/solution.py
@@ -50,9 +50,19 @@
     return jax.nn.silu(normed * gain + shift).astype(jnp.bfloat16)
 
 
-def level3_totals(values, group_width):
-    sums, squares = moments(values, group_width)
-    return lax.psum((sums, squares), "rows")
+def totals(vector):
+    names = ("rows", "cols")
+    count = lax.axis_size(names)
+    copies = jnp.broadcast_to(vector, (count,) + vector.shape)
+    return jnp.sum(lax.all_to_all(copies, names, 0, 0), axis=0)
+
+
+def inside(height, width):
+    row = lax.axis_index("rows") * height - 2 + jnp.arange(height + 4, dtype=jnp.int32)
+    col = lax.axis_index("cols") * width - 2 + jnp.arange(width + 4, dtype=jnp.int32)
+    row_ok = (row >= 0) & (row < height * lax.axis_size("rows"))
+    col_ok = (col >= 0) & (col < width * lax.axis_size("cols"))
+    return (row_ok[:, None] & col_ok[None, :])[:, :, None]
 
 
 def folder(kernel, total, piece):
@@ -90,39 +100,53 @@
     cols_one = latent1.shape[1]
     width_one = C1 // 32
     count_one = rows_one * cols_one * lax.axis_size("rows") * lax.axis_size("cols") * width_one
-    sums, squares = moments(latent1, width_one)
-    sums, squares = lax.psum((sums, squares), ("rows", "cols"))
-    act1 = normalize(latent1, sums, squares, count_one, norm1a_g, norm1a_b)
-    padded = extended(act1, (("rows", 0), ("cols", 1)), 1)
-    hid1 = conv_valid(padded, conv1a_w)
-    sums_two, squares_two = moments(hid1, width_one)
-    sums_two, squares_two = lax.psum((sums_two, squares_two), ("rows", "cols"))
-    act2 = normalize(hid1, sums_two, squares_two, count_one, norm1b_g, norm1b_b)
-    padded_two = extended(act2, (("rows", 0), ("cols", 1)), 1)
-    out1 = (latent1.astype(jnp.float32) + conv_valid(padded_two, conv1b_w) + conv1b_b).astype(
-        jnp.bfloat16
-    )
     joined = (feat3.astype(jnp.float32) + adapter3.astype(jnp.float32)).astype(jnp.bfloat16)
     shard = conv3a_w.shape[3]
     height = feat3.shape[0]
     width = feat3.shape[1] * lax.axis_size("cols")
     width_three = C3 // 32
     count_three = height * width * lax.axis_size("rows") * width_three
-    empty = jnp.zeros((height, width, shard), jnp.float32)
+    zero = jnp.zeros((), jnp.bfloat16)
+    raw = extended(latent1, (("rows", 0), ("cols", 1)), 2)
     edged_tile = extended(joined, (("rows", 0),), 1)
     whole = lax.all_gather(edged_tile, "cols", axis=1, tiled=True)
+    first = totals(jnp.concatenate(moments(latent1, width_one) + moments(joined, width_three)))
+    sums, squares, sums_three, squares_three = jnp.split(first, 4)
+    ok = inside(rows_one, cols_one)
+    act1 = jnp.where(ok, normalize(raw, sums, squares, count_one, norm1a_g, norm1a_b), zero)
+    hid1 = conv_valid(act1, conv1a_w)
     local = lax.dynamic_slice_in_dim(whole[1:-1], lax.axis_index("cols") * shard, shard, 2)
-    sums_three, squares_three = level3_totals(whole[1:-1], width_three)
     line_ids = lax.axis_index("rows") * height - 1 + jnp.arange(height + 2, dtype=jnp.int32)
     line_ok = (line_ids >= 0) & (line_ids < height * lax.axis_size("rows"))
     act_whole = normalize(whole, sums_three, squares_three, count_three, norm3a_g, norm3a_b)
-    act_whole = jnp.where(line_ok[:, None, None], act_whole, jnp.zeros((), jnp.bfloat16))
+    act_whole = jnp.where(line_ok[:, None, None], act_whole, zero)
     hid3 = conv_valid(jnp.pad(act_whole, ((0, 0), (1, 1), (0, 0))), conv3a_w)
-    sums_four, squares_four = moments(hid3, width_three)
-    sums_four, squares_four = lax.psum((sums_four, squares_four), "rows")
-    act4 = normalize(hid3, sums_four, squares_four, count_three, norm3b_g, norm3b_b)
+    pieces = moments(hid3, width_three)
+    spread = [
+        jnp.where(
+            jnp.arange(32) // part.shape[0] == lax.axis_index("cols"), jnp.tile(part, 32 // part.shape[0]), 0.0
+        )
+        for part in pieces
+    ]
+    second_sums = totals(jnp.concatenate(moments(hid1[1:-1, 1:-1], width_one) + tuple(spread)))
+    sums_two, squares_two, sums_four, squares_four = jnp.split(second_sums, 4)
+    own = shard // width_three
+    start = lax.axis_index("cols") * own
+    act4 = normalize(
+        hid3,
+        lax.dynamic_slice_in_dim(sums_four, start, own),
+        lax.dynamic_slice_in_dim(squares_four, start, own),
+        count_three,
+        norm3b_g,
+        norm3b_b,
+    )
     edged_two = extended(act4, (("rows", 0),), 1)
-    second = folder(conv3b_w, empty, lax.all_gather(edged_two, "cols", axis=2, tiled=True))
+    whole_two = lax.all_gather(edged_two, "cols", axis=2, tiled=True)
+    act2 = normalize(hid1, sums_two, squares_two, count_one, norm1b_g, norm1b_b)
+    act2 = jnp.where(ok[1:-1, 1:-1], act2, zero)
+    out1 = (latent1.astype(jnp.float32) + conv_valid(act2, conv1b_w) + conv1b_b).astype(jnp.bfloat16)
+    empty = jnp.zeros((height, width, shard), jnp.float32)
+    second = folder(conv3b_w, empty, whole_two)
     out3 = (local.astype(jnp.float32) + second + conv3b_b).astype(jnp.bfloat16)
     return (out1, out3)
 

time: 273 us -> 146 us (0.53); the launches traced: 268 us -> 145 us
  blocking collectives: 103 us -> 0 us
  waiting for transfers between devices: 37.3 us -> 14.5 us
    psum x4 -> x0, blocking collectives: 103 us -> none  [the longest x1 44.7 us: body(): sums_two, squares_two = lax.psum((sums_two, squares_two), ('rows', 'cols'))]
    all_gather x1, waiting for transfers between devices: 26.1 us -> 0.02 us  [body(): whole = lax.all_gather(edged_tile, 'cols', axis=1, tiled=True)]
    all_to_all x0 -> x2, starting transfers between devices: none -> 12.1 us  [totals(): return jnp.sum(lax.all_to_all(copies, names, 0, 0), axis=0)]
    all_to_all x0 -> x2, waiting for transfers between devices: none -> 10 us  [totals(): return jnp.sum(lax.all_to_all(copies, names, 0, 0), axis=0)]
    ppermute x6 -> x4, waiting for transfers between devices: 9.13 us -> 0.05 us  [extended(): lax.ppermute(lax.slice_in_dim(block, 0, width, axis=dim), axis, backward)]
    ppermute x6 -> x4, starting transfers between devices: 19.6 us -> 12.8 us  [extended(): lax.ppermute(lax.slice_in_dim(block, 0, width, axis=dim), axis, backward)]
    conv_general_dilated x11, local copies, waits for them, and re-layouts: 9.39 us -> 6.31 us  [conv_valid(): lax.conv_general_dilated(padded[None], kernel, (1, 1), 'VALID', dimension...]
    ppermute x6 -> x4, starting transfers between devices: 13.2 us -> 10.5 us  [extended(): lax.ppermute(lax.slice_in_dim(block, block.shape[dim] - width, None, axis...]
  transfers between devices with their start and end apart: 14 -> 12, of which waited for: 8 -> 4; matrix products, arithmetic and copies ran while one was open for 14% -> 33% of each run, Pallas kernels for 0% -> 0%
where the time goes in v1:
time: 146 us; the launch traced here: 145 us
  local copies, waits for them, and re-layouts  46.6 us (32%)
  starting transfers between devices  35.5 us (24%)
  other arithmetic  17.8 us (12%)
  matrix products  16.2 us (11%)
  between operations  14.8 us (10%)
  waiting for transfers between devices  14.5 us (10%)
    unnamed x71, local copies, waits for them, and re-layouts  16.8 us
    ppermute x4, starting transfers between devices, extended(): lax.ppermute(lax.slice_in_dim(block, 0, width, axis=dim), axis, backward)  12.8 us
    all_to_all x2, starting transfers between devices, totals(): return jnp.sum(lax.all_to_all(copies, names, 0, 0), axis=0)  12.1 us
    conv_general_dilated x3, matrix products, conv_valid(): lax.conv_general_dilated(padded[None], kernel, (1, 1), 'VALID', dimension...  11.6 us
    ppermute x4, starting transfers between devices, extended(): lax.ppermute(lax.slice_in_dim(block, block.shape[dim] - width, None, axis...  10.5 us
    all_to_all x2, waiting for transfers between devices, totals(): return jnp.sum(lax.all_to_all(copies, names, 0, 0), axis=0)  10 us
    reshape x1, local copies, waits for them, and re-layouts, folder(): weights = kernel.reshape(9 * count, kernel.shape[3])  9.39 us
    conv_general_dilated x11, local copies, waits for them, and re-layouts, conv_valid(): lax.conv_general_dilated(padded[None], kernel, (1, 1), 'VALID', dimension...  6.31 us
  transfers between devices with their start and end apart: 12, of which 4 were waited for; matrix products, arithmetic and copies ran while one was open for 33% of the time, Pallas kernels for 0%

profile of v1, /device:TPU:4, one launch (start us, length us, event | category | flops | bytes accessed | tf_op | source)
XLA Modules:
  0.0 145.4 jit_solution(1666216868696391539)
XLA Ops:
  7.2 1.9 %convert_reduce_fusion.1 = (f32[1280]{0:T(1024)}, f32[1280]{0:T(1024)}, bf16[4,16,1280]{2,1,0:T(8,128)(2,1)S(1)}) fusion(bf16[4,16,1280]{2,1,0:T(8,128)(2,1)} %param.26, bf16[4,16,1280]{2,1,0:T(8,128)(2,1)} %param.25), kind=kLoop, calls=%fused_computation.61 | loop fusion | flops 652800 | bytes 501760 | tf_op jit(solution)/shard_map/reduce_sum | solution.py:40
  9.1 0.6 fusion.52
  9.7 3.3 %collective-permute-start.5 = (bf16[1,16,1280]{2,1,0:T(8,128)(2,1)}, bf16[1,16,1280]{2,1,0:T(8,128)(2,1)}, u32[]{:S(2)}, u32[]{:S(2)}) collective-permute-start(bf16[1,16,1280]{2,1,0:T(8,128)(2,1)} %get-tuple-element.30), channel_id=1, source_target_pairs={{8,0},{16,8},{24,16},{9,1},{17,9},{25,17},{10,2},{18,10},{26,18},{... | collective-permute-start | bytes 122888 | tf_op jit(solution)/shard_map/ppermute | solution.py:21
  13.1 3.1 %collective-permute-start.4 = (bf16[1,16,1280]{2,1,0:T(8,128)(2,1)}, bf16[1,16,1280]{2,1,0:T(8,128)(2,1)}, u32[]{:S(2)}, u32[]{:S(2)}) collective-permute-start(bf16[1,16,1280]{2,1,0:T(8,128)(2,1)} %get-tuple-element.29), channel_id=1, source_target_pairs={{0,8},{8,16},{16,24},{1,9},{9,17},{17,25},{2,10},{10,18},{18,26},{... | collective-permute-start | bytes 122888 | tf_op jit(solution)/shard_map/ppermute | solution.py:18
  16.2 1.0 fusion.50
  17.1 1.9 %collective-permute-start = (bf16[2,64,320]{2,1,0:T(8,128)(2,1)S(1)}, bf16[2,64,320]{2,1,0:T(8,128)(2,1)S(1)}, u32[]{:S(2)}, u32[]{:S(2)}) collective-permute-start(bf16[2,64,320]{2,1,0:T(8,128)(2,1)S(1)} %get-tuple-element.26), channel_id=1, source_target_pairs={{0,8},{8,16},{16,24},{1,9},{9,17},{17,25},{2,10},{10,18},{18,26},{... | collective-permute-start | bytes 245768 | tf_op jit(solution)/shard_map/ppermute | solution.py:18
  19.1 4.8 %collective-permute-start.1 = (bf16[2,64,320]{2,1,0:T(8,128)(2,1)S(1)}, bf16[2,64,320]{2,1,0:T(8,128)(2,1)S(1)}, u32[]{:S(2)}, u32[]{:S(2)}) collective-permute-start(bf16[2,64,320]{2,1,0:T(8,128)(2,1)S(1)} %get-tuple-element.25), channel_id=1, source_target_pairs={{8,0},{16,8},{24,16},{9,1},{17,9},{25,17},{10,2},{18,10},{26,18},{... | collective-permute-start | bytes 245768 | tf_op jit(solution)/shard_map/ppermute | solution.py:21
  23.9 1.4 reduce_sum.127
  25.3 1.4 reduce_sum.121
  26.7 1.4 reduce_sum.128
  28.0 1.4 reduce_sum.122
  29.4 1.5 %pad_maximum_fusion = bf16[6,16,1280]{2,1,0:T(8,128)(2,1)} fusion(bf16[1,16,1280]{2,1,0:T(8,128)(2,1)} %collective-permute-done.5, bf16[4,16,1280]{2,1,0:T(8,128)(2,1)S(1)} %get-tuple-element.22, bf16[1,16,1280]{2,1,0:T(8,128)(2,1)} %collective-permute-done.4), kind=kLoop, calls=%fused_computation.69 | loop fusion | flops 245760 | bytes 491520 | tf_op jit(solution)/shard_map/concatenate | solution.py:22
  31.0 0.5 convert_reduce_fusion
  31.9 0.7 pad_maximum_fusion.2
  32.6 0.6 broadcast_in_dim.71
  33.2 5.2 %all-to-all-start = ((f32[32,1,128]{2,1,0:T(1,128)}), f32[32,1,128]{2,1,0:T(1,128)S(1)}, u32[]{:S(2)}, u32[]{:S(2)}) async-start(f32[32,1,128]{2,1,0:T(1,128)} %broadcast_in_dim.71), calls=%async_computation | async-start | bytes 32768 | tf_op jit(solution)/shard_map/all_to_all | solution.py:57
  38.5 0.7 broadcast_and_fusion
  39.1 0.5 compare_and_fusion
  39.7 4.7 %all-to-all-done = f32[32,1,128]{2,1,0:T(1,128)S(1)} async-done(((f32[32,1,128]{2,1,0:T(1,128)}), f32[32,1,128]{2,1,0:T(1,128)S(1)}, u32[]{:S(2)}, u32[]{:S(2)}) %all-to-all-start) | async-done | bytes 16416 | tf_op jit(solution)/shard_map/all_to_all | solution.py:57
  44.6 1.0 copy-done.6
  45.6 1.3 collective-permute-start.3
  47.0 3.0 %collective-permute-start.2 = (bf16[20,2,320]{2,1,0:T(2,128)(2,1)S(1)}, bf16[20,2,320]{2,1,0:T(2,128)(2,1)S(1)}, u32[]{:S(2)}, u32[]{:S(2)}) collective-permute-start(bf16[20,2,320]{2,1,0:T(2,128)(2,1)S(1)} %get-tuple-element.23), channel_id=1, source_target_pairs={{0,1},{1,2},{2,3},{3,4},{4,5},{5,6},{6,7},{8,9},{9,10},{10,11},{11... | collective-permute-start | bytes 76808 | tf_op jit(solution)/shard_map/ppermute | solution.py:18
  50.8 2.3 %fusion.33 = bf16[20,1,68,320]{3,2,0,1:T(8,128)(2,1)S(1)} fusion(bf16[1,20,2,320]{3,2,1,0:T(2,128)(2,1)S(1)} %bitcast.66, bf16[1,20,64,320]{3,2,1,0:T(8,128)(2,1)} %bitcast.63, bf16[1,20,2,320]{3,2,1,0:T(2,128)(2,1)S(1)} %bitcast.67, f32[320]{0:T(512)S(1)} %copy-done.10, f32[320]{0:T(512)S(1)} %copy-done.11, f32[320]{0:T(512)S(1)} %mul.173, f32[320]{0:T(512)S(1)} %sub.92, ...), kind=kLoop, calls=%fused_computation.55 | loop fusion | flops 6963200 | bytes 1747280 | tf_op jit(solution)/shard_map/jit(_where)/select_n | solution.py:116
  53.8 0.3 copy-done.27
  54.1 4.3 %convolution_select_fusion = f32[18,8,9,320]{3,1,2,0:T(8,128)S(1)} fusion(bf16[3,3,320,320]{3,2,1,0:T(8,128)(2,1)S(1)} %copy-done, bf16[20,1,7,2,320]{4,2,3,0,1:T(8,128)(2,1)S(1)} %slice.94, bf16[20,1,8,9,320]{4,2,3,0,1:T(8,128)(2,1)S(1)} %copy.137, pred[8,9]{0,1:T(8,128)(4,1)S(1)} %copy-done.27), kind=kOutput, calls=%fused_computation.26 | convolution fusion | flops 2392581120 | bytes 4602952 | tf_op jit(solution)/shard_map/conv_general_dilated | solution.py:27
  58.4 0.5 copy.138
  58.9 0.9 copy-done.3
  59.9 0.3 slice_reduce_fusion
  60.7 3.0 %fusion.10 = bf16[6,128,1280]{2,1,0:T(8,128)(2,1)S(1)} fusion(bf16[6,128,1280]{2,1,0:T(8,128)(2,1)} %all-gather.3.cloned.1.call-done, f32[1280]{0:T(1024)S(1)} %copy-done.8, f32[1280]{0:T(1024)S(1)} %copy-done.9, f32[1280]{0:T(1024)S(1)} %mul.183, f32[1280]{0:T(1024)S(1)} %sub.99, pred[6]{0:T(512)(128)(4,1)S(1)} %copy-done.17), kind=kLoop, calls=%fused_computation.20 | loop fusion | flops 10813440 | bytes 3952646 | tf_op jit(solution)/shard_map/jit(_where)/select_n | solution.py:122
  63.8 0.5 pad_bitcast_fusion
  64.4 2.4 %reshape.235 = bf16[6,1,8,17,1280]{4,3,2,0,1:T(8,128)(2,1)} reshape(bf16[6,1,136,1280]{3,2,0,1:T(8,128)(2,1)S(1)} %pad.11) | data formatting | bytes 4177920 | tf_op jit(solution)/shard_map/conv_general_dilated | solution.py:27
  66.8 2.4 %copy.140 = bf16[6,1,8,17,1280]{4,2,3,0,1:T(8,128)(2,1)S(1)} copy(bf16[6,1,8,17,1280]{4,3,2,0,1:T(8,128)(2,1)} %reshape.235) | data formatting | bytes 4177920 | tf_op jit(solution)/shard_map/conv_general_dilated | solution.py:27
  69.3 0.5 copy-done.22
  69.7 3.5 %select_reduce_fusion.1 = (f32[160]{0:T(256)S(1)}, f32[160]{0:T(256)S(1)}, f32[4,8,17,160]{3,1,2,0:T(8,128)S(1)}) fusion(pred[8,17]{0,1:T(8,128)(4,1)S(1)} %copy-done.25, bf16[3,3,1280,160]{2,3,1,0:T(8,128)(2,1)S(1)} %copy-done.22, bf16[6,1,7,2,1280]{4,2,3,0,1:T(8,128)(2,1)S(1)} %slice.99, bf16[6,1,8,17,1280]{4,2,3,0,1:T(8,128)(2,1)S(1)} %copy.140), kind=kOutput, calls=%fused_computation.59 | convolution fusion | flops 2012927744 | bytes 6339976 | tf_op jit(solution)/shard_map/conv_general_dilated | solution.py:27
  73.9 0.6 broadcast_in_dim.77
  74.6 7.0 %all-to-all-start.1 = ((f32[32,1,128]{2,1,0:T(1,128)}), f32[32,1,128]{2,1,0:T(1,128)S(1)}, u32[]{:S(2)}, u32[]{:S(2)}) async-start(f32[32,1,128]{2,1,0:T(1,128)} %broadcast_in_dim.77), calls=%async_computation.1 | async-start | bytes 32768 | tf_op jit(solution)/shard_map/all_to_all | solution.py:57
  81.6 0.2 copy.147
  81.9 0.2 copy.157
  82.1 5.4 %all-to-all-done.1 = f32[32,1,128]{2,1,0:T(1,128)S(1)} async-done(((f32[32,1,128]{2,1,0:T(1,128)}), f32[32,1,128]{2,1,0:T(1,128)S(1)}, u32[]{:S(2)}, u32[]{:S(2)}) %all-to-all-start.1) | async-done | bytes 16416 | tf_op jit(solution)/shard_map/all_to_all | solution.py:57
  88.0 0.2 multiply_convert_fusion.3
  88.2 3.4 %collective-permute-start.7 = (bf16[1,128,160]{1,2,0:T(8,128)(2,1)S(1)}, bf16[1,128,160]{1,2,0:T(8,128)(2,1)S(1)}, u32[]{:S(2)}, u32[]{:S(2)}) collective-permute-start(bf16[1,128,160]{1,2,0:T(8,128)(2,1)S(1)} %get-tuple-element.28), channel_id=1, source_target_pairs={{8,0},{16,8},{24,16},{9,1},{17,9},{25,17},{10,2},{18,10},{26,18},{... | collective-permute-start | bytes 122888 | tf_op jit(solution)/shard_map/ppermute | solution.py:21
  91.6 2.5 %collective-permute-start.6 = (bf16[1,128,160]{1,2,0:T(8,128)(2,1)S(1)}, bf16[1,128,160]{1,2,0:T(8,128)(2,1)S(1)}, u32[]{:S(2)}, u32[]{:S(2)}) collective-permute-start(bf16[1,128,160]{1,2,0:T(8,128)(2,1)S(1)} %get-tuple-element.27), channel_id=1, source_target_pairs={{0,8},{8,16},{16,24},{1,9},{9,17},{17,25},{2,10},{10,18},{18,26},{... | collective-permute-start | bytes 122888 | tf_op jit(solution)/shard_map/ppermute | solution.py:18
  94.1 4.3 %collective-permute-done.6 = bf16[1,128,160]{1,2,0:T(8,128)(2,1)S(1)} collective-permute-done((bf16[1,128,160]{1,2,0:T(8,128)(2,1)S(1)}, bf16[1,128,160]{1,2,0:T(8,128)(2,1)S(1)}, u32[]{:S(2)}, u32[]{:S(2)}) %collective-permute-start.6) | collective-permute-done | bytes 40992 | tf_op jit(solution)/shard_map/ppermute | solution.py:18
  98.4 0.7 pad_maximum_fusion.1
  99.5 7.4 %copy.153 = bf16[3,3,1280,160]{2,1,0,3:T(4,128)(2,1)} copy(bf16[3,3,1280,160]{2,3,1,0:T(8,128)(2,1)} %param.32) | data formatting | bytes 7372800 | tf_op args[15]
  106.9 9.4 %reshape.271 = bf16[11520,160,1]{0,1,2:T(8,128)(2,1)} reshape(bf16[3,3,1280,160]{2,1,0,3:T(4,128)(2,1)} %copy.153) | data formatting | bytes 7372800 | tf_op jit(solution)/shard_map/reshape | solution.py:75
  116.3 1.6 %slice.103 = bf16[4,128,1280]{2,1,0:T(8,128)(2,1)S(1)} slice(bf16[6,128,1280]{2,1,0:T(8,128)(2,1)} %all-gather.3.cloned.1.call-done), slice={[1:5], [0:128], [0:1280]} | slice | bytes 2621440 | tf_op jit(solution)/shard_map/slice | solution.py:118
  118.6 0.6 multiply_convert_fusion.2
  119.4 0.3 slice_select_fusion
  120.1 1.3 copy-done.23
  121.4 3.8 %convolution_select_fusion.1 = f32[16,8,9,320]{3,1,2,0:T(8,128)S(1)} fusion(bf16[3,3,320,320]{3,2,1,0:T(8,128)(2,1)S(1)} %copy-done.23, bf16[18,1,7,2,320]{4,2,3,0,1:T(8,128)(2,1)S(1)} %slice.101, bf16[18,1,8,9,320]{4,2,3,0,1:T(8,128)(2,1)S(1)} %copy.144, pred[8,9]{0,1:T(8,128)(4,1)S(1)} %copy-done.26), kind=kOutput, calls=%fused_computation.28 | convolution fusion | flops 2126776320 | bytes 4308552 | tf_op jit(solution)/shard_map/conv_general_dilated | solution.py:27
  125.2 0.3 copy.145
  125.5 0.3 copy-done.14
  125.9 0.5 fusion.13
  126.4 1.1 copy.154
  127.5 2.7 %copy.149 = bf16[6,128,1280]{2,1,0:T(8,128)(2,1)S(1)} copy(bf16[6,128,1280]{1,2,0:T(8,128)(2,1)} %all-gather.5.cloned.1.call-done) | data formatting | bytes 3932160 | tf_op jit(solution)/shard_map/all_gather | solution.py:144
  130.1 0.3 slice_dynamic-update-slice_fusion.8
  130.5 0.3 slice_dynamic-update-slice_fusion.7
  130.9 0.3 slice_dynamic-update-slice_fusion.6
  131.3 0.3 slice_dynamic-update-slice_fusion.5
  131.6 0.3 slice_dynamic-update-slice_fusion.4
  132.0 0.3 slice_dynamic-update-slice_fusion.3
  132.3 1.6 %copy-done.5 = bf16[11520,160,1]{0,1,2:T(8,128)(2,1)S(1)} copy-done((bf16[11520,160,1]{0,1,2:T(8,128)(2,1)S(1)}, bf16[11520,160,1]{0,1,2:T(8,128)(2,1)}, u32[]{:S(2)}) %copy-start.5) | copy-done | bytes 3686424
  133.9 4.6 %fusion.31 = bf16[4,128,160]{1,2,0:T(8,128)(2,1)} fusion(bf16[4,128,11520]{2,1,0:T(8,128)(2,1)S(1)} %slice_dynamic-update-slice_fusion.3, bf16[11520,160,1]{0,1,2:T(8,128)(2,1)S(1)} %copy-done.5, bf16[4,128,160]{1,2,0:T(8,128)(2,1)S(1)} %copy.156, f32[160]{0:T(256)S(1)} %copy-done.24), kind=kOutput, calls=%fused_computation.53 | convolution fusion | flops 1887764480 | bytes 15811200 | tf_op jit(solution)/shard_map/dot_general | solution.py:76
  (129 shorter events, 6.2 us)
Async XLA Ops:
  7.2 46.6 %copy-start = (bf16[3,3,320,320]{3,2,1,0:T(8,128)(2,1)S(1)}, bf16[3,3,320,320]{3,2,1,0:T(8,128)(2,1)}, u32[]{:S(2)}) copy-start(bf16[3,3,320,320]{3,2,1,0:T(8,128)(2,1)} %param.20) | copy-start | bytes 5529604
  7.2 23.8 %copy-start.2 = (bf16[16,64,320]{2,1,0:T(8,128)(2,1)S(1)}, bf16[16,64,320]{2,1,0:T(8,128)(2,1)}, u32[]{:S(2)}) copy-start(bf16[16,64,320]{2,1,0:T(8,128)(2,1)} %param.17) | copy-start | bytes 1966084
  7.2 53.5 %all-gather.3.cloned.1.call-start = ((), (), s32[]{:S(2)}) async-start(), calls=%async_computation.2 | async-start | bytes 2211840 | tf_op jit(solution)/shard_map/all_gather | solution.py:112
  9.7 19.7 %collective-permute-start.5 = (bf16[1,16,1280]{2,1,0:T(8,128)(2,1)}, bf16[1,16,1280]{2,1,0:T(8,128)(2,1)}, u32[]{:S(2)}, u32[]{:S(2)}) collective-permute-start(bf16[1,16,1280]{2,1,0:T(8,128)(2,1)} %get-tuple-element.30), channel_id=1, source_target_pairs={{8,0},{16,8},{24,16},{9,1},{17,9},{25,17},{10,2},{18,10},{26,18},{... | collective-permute-start | bytes 122888 | tf_op jit(solution)/shard_map/ppermute | solution.py:21
  13.1 16.3 %collective-permute-start.4 = (bf16[1,16,1280]{2,1,0:T(8,128)(2,1)}, bf16[1,16,1280]{2,1,0:T(8,128)(2,1)}, u32[]{:S(2)}, u32[]{:S(2)}) collective-permute-start(bf16[1,16,1280]{2,1,0:T(8,128)(2,1)} %get-tuple-element.29), channel_id=1, source_target_pairs={{0,8},{8,16},{16,24},{1,9},{9,17},{17,25},{2,10},{10,18},{18,26},{... | collective-permute-start | bytes 122888 | tf_op jit(solution)/shard_map/ppermute | solution.py:18
  17.1 27.2 %collective-permute-start = (bf16[2,64,320]{2,1,0:T(8,128)(2,1)S(1)}, bf16[2,64,320]{2,1,0:T(8,128)(2,1)S(1)}, u32[]{:S(2)}, u32[]{:S(2)}) collective-permute-start(bf16[2,64,320]{2,1,0:T(8,128)(2,1)S(1)} %get-tuple-element.26), channel_id=1, source_target_pairs={{0,8},{8,16},{16,24},{1,9},{9,17},{17,25},{2,10},{10,18},{18,26},{... | collective-permute-start | bytes 245768 | tf_op jit(solution)/shard_map/ppermute | solution.py:18
  19.1 25.5 %collective-permute-start.1 = (bf16[2,64,320]{2,1,0:T(8,128)(2,1)S(1)}, bf16[2,64,320]{2,1,0:T(8,128)(2,1)S(1)}, u32[]{:S(2)}, u32[]{:S(2)}) collective-permute-start(bf16[2,64,320]{2,1,0:T(8,128)(2,1)S(1)} %get-tuple-element.25), channel_id=1, source_target_pairs={{8,0},{16,8},{24,16},{9,1},{17,9},{25,17},{10,2},{18,10},{26,18},{... | collective-permute-start | bytes 245768 | tf_op jit(solution)/shard_map/ppermute | solution.py:21
  33.2 11.1 %all-to-all-start = ((f32[32,1,128]{2,1,0:T(1,128)}), f32[32,1,128]{2,1,0:T(1,128)S(1)}, u32[]{:S(2)}, u32[]{:S(2)}) async-start(f32[32,1,128]{2,1,0:T(1,128)} %broadcast_in_dim.71), calls=%async_computation | async-start | bytes 32768 | tf_op jit(solution)/shard_map/all_to_all | solution.py:57
  38.4 5.9 %copy-start.18 = (pred[68]{0:T(512)(128)(4,1)}, pred[68]{0:T(512)(128)(4,1)S(1)}, u32[]{:S(2)}) copy-start(pred[68]{0:T(512)(128)(4,1)S(1)} %compare_and_fusion.1) | copy-start | bytes 208
  38.5 8.5 %copy-start.20 = (pred[20]{0:T(512)(128)(4,1)}, pred[20]{0:T(512)(128)(4,1)S(1)}, u32[]{:S(2)}) copy-start(pred[20]{0:T(512)(128)(4,1)S(1)} %compare_and_fusion.2) | copy-start | bytes 64
  44.4 6.5 %copy-start.7 = (pred[20,68]{1,0:T(8,128)(4,1)S(1)}, pred[20,68]{1,0:T(8,128)(4,1)}, u32[]{:S(2)}) copy-start(pred[20,68]{1,0:T(8,128)(4,1)} %broadcast_and_fusion) | copy-start | bytes 4084
  44.4 6.5 %copy-start.10 = (f32[320]{0:T(512)S(1)}, f32[320]{0:T(512)}, u32[]{:S(2)}) copy-start(f32[320]{0:T(512)} %param.19) | copy-start | bytes 3844
  44.4 6.5 %copy-start.11 = (f32[320]{0:T(512)S(1)}, f32[320]{0:T(512)}, u32[]{:S(2)}) copy-start(f32[320]{0:T(512)} %param.18) | copy-start | bytes 3844
  44.6 1.0 copy-start.6
  45.6 5.1 %collective-permute-start.3 = (bf16[20,2,320]{2,1,0:T(2,128)(2,1)S(1)}, bf16[20,2,320]{2,1,0:T(2,128)(2,1)S(1)}, u32[]{:S(2)}, u32[]{:S(2)}) collective-permute-start(bf16[20,2,320]{2,1,0:T(2,128)(2,1)S(1)} %get-tuple-element.24), channel_id=1, source_target_pairs={{1,0},{2,1},{3,2},{4,3},{5,4},{6,5},{7,6},{9,8},{10,9},{11,10},{12... | collective-permute-start | bytes 76808 | tf_op jit(solution)/shard_map/ppermute | solution.py:21
  47.0 3.9 %collective-permute-start.2 = (bf16[20,2,320]{2,1,0:T(2,128)(2,1)S(1)}, bf16[20,2,320]{2,1,0:T(2,128)(2,1)S(1)}, u32[]{:S(2)}, u32[]{:S(2)}) collective-permute-start(bf16[20,2,320]{2,1,0:T(2,128)(2,1)S(1)} %get-tuple-element.23), channel_id=1, source_target_pairs={{0,1},{1,2},{2,3},{3,4},{4,5},{5,6},{6,7},{8,9},{9,10},{10,11},{11... | collective-permute-start | bytes 76808 | tf_op jit(solution)/shard_map/ppermute | solution.py:18
  53.4 0.7 copy-start.27
  58.4 1.3 copy-start.3
  59.7 1.0 copy-start.8
  59.7 1.0 copy-start.9
  59.7 1.0 copy-start.17
  66.8 2.9 %copy-start.22 = (bf16[3,3,1280,160]{2,3,1,0:T(8,128)(2,1)S(1)}, bf16[3,3,1280,160]{2,3,1,0:T(8,128)(2,1)}, u32[]{:S(2)}) copy-start(bf16[3,3,1280,160]{2,3,1,0:T(8,128)(2,1)} %param.29) | copy-start | bytes 11059204
  66.8 2.9 %copy-start.25 = (pred[8,17]{0,1:T(8,128)(4,1)S(1)}, pred[8,17]{0,1:T(8,128)(4,1)}, u32[]{:S(2)}) copy-start(pred[8,17]{0,1:T(8,128)(4,1)} %constant.103) | copy-start | bytes 412
  73.2 14.7 %copy-start.15 = (f32[160]{0:T(256)S(1)}, f32[160]{0:T(256)}, u32[]{:S(2)}) copy-start(f32[160]{0:T(256)} %param.31) | copy-start | bytes 1924
  73.3 14.7 %copy-start.16 = (f32[160]{0:T(256)S(1)}, f32[160]{0:T(256)}, u32[]{:S(2)}) copy-start(f32[160]{0:T(256)} %param.30) | copy-start | bytes 1924
  74.6 12.9 %all-to-all-start.1 = ((f32[32,1,128]{2,1,0:T(1,128)}), f32[32,1,128]{2,1,0:T(1,128)S(1)}, u32[]{:S(2)}, u32[]{:S(2)}) async-start(f32[32,1,128]{2,1,0:T(1,128)} %broadcast_in_dim.77), calls=%async_computation.1 | async-start | bytes 32768 | tf_op jit(solution)/shard_map/all_to_all | solution.py:57
  81.5 45.9 %all-gather.5.cloned.1.call-start = ((), (), s32[]{:S(2)}) async-start(), calls=%async_computation.3 | async-start | bytes 2211840 | tf_op jit(solution)/shard_map/all_gather | solution.py:144
  81.6 17.5 %copy-start.19 = (pred[68]{0:T(512)(128)(4,1)S(1)}, pred[68]{0:T(512)(128)(4,1)}, u32[]{:S(2)}) copy-start(pred[68]{0:T(512)(128)(4,1)} %copy-done.18) | copy-start | bytes 208
  81.6 17.6 %copy-start.21 = (pred[20]{0:T(512)(128)(4,1)S(1)}, pred[20]{0:T(512)(128)(4,1)}, u32[]{:S(2)}) copy-start(pred[20]{0:T(512)(128)(4,1)} %copy-done.20) | copy-start | bytes 64
  88.2 5.9 %collective-permute-start.7 = (bf16[1,128,160]{1,2,0:T(8,128)(2,1)S(1)}, bf16[1,128,160]{1,2,0:T(8,128)(2,1)S(1)}, u32[]{:S(2)}, u32[]{:S(2)}) collective-permute-start(bf16[1,128,160]{1,2,0:T(8,128)(2,1)S(1)} %get-tuple-element.28), channel_id=1, source_target_pairs={{8,0},{16,8},{24,16},{9,1},{17,9},{25,17},{10,2},{18,10},{26,18},{... | collective-permute-start | bytes 122888 | tf_op jit(solution)/shard_map/ppermute | solution.py:21
  91.6 6.8 %collective-permute-start.6 = (bf16[1,128,160]{1,2,0:T(8,128)(2,1)S(1)}, bf16[1,128,160]{1,2,0:T(8,128)(2,1)S(1)}, u32[]{:S(2)}, u32[]{:S(2)}) collective-permute-start(bf16[1,128,160]{1,2,0:T(8,128)(2,1)S(1)} %get-tuple-element.27), channel_id=1, source_target_pairs={{0,8},{8,16},{16,24},{1,9},{9,17},{17,25},{2,10},{10,18},{18,26},{... | collective-permute-start | bytes 122888 | tf_op jit(solution)/shard_map/ppermute | solution.py:18
  116.3 2.3 %copy-start.4 = (f32[18,8,9,320]{3,1,2,0:T(8,128)S(1)}, f32[18,8,9,320]{3,1,2,0:T(8,128)}, u32[]{:S(2)}) copy-start(f32[18,8,9,320]{3,1,2,0:T(8,128)} %copy-done.3) | copy-start | bytes 4976644
  116.3 2.3 %copy-start.12 = (f32[320]{0:T(512)S(1)}, f32[320]{0:T(512)}, u32[]{:S(2)}) copy-start(f32[320]{0:T(512)} %param.22) | copy-start | bytes 3844
  116.3 2.3 %copy-start.13 = (f32[320]{0:T(512)S(1)}, f32[320]{0:T(512)}, u32[]{:S(2)}) copy-start(f32[320]{0:T(512)} %param.21) | copy-start | bytes 3844
  119.7 1.6 %copy-start.23 = (bf16[3,3,320,320]{3,2,1,0:T(8,128)(2,1)S(1)}, bf16[3,3,320,320]{3,2,1,0:T(8,128)(2,1)}, u32[]{:S(2)}) copy-start(bf16[3,3,320,320]{3,2,1,0:T(8,128)(2,1)} %param.23) | copy-start | bytes 5529604
  119.7 1.6 %copy-start.26 = (pred[8,9]{0,1:T(8,128)(4,1)S(1)}, pred[8,9]{0,1:T(8,128)(4,1)}, u32[]{:S(2)}) copy-start(pred[8,9]{0,1:T(8,128)(4,1)} %constant.101) | copy-start | bytes 220
  125.2 0.7 copy-start.14
  131.9 2.0 %copy-start.5 = (bf16[11520,160,1]{0,1,2:T(8,128)(2,1)S(1)}, bf16[11520,160,1]{0,1,2:T(8,128)(2,1)}, u32[]{:S(2)}) copy-start(bf16[11520,160,1]{0,1,2:T(8,128)(2,1)} %reshape.271) | copy-start | bytes 11059204
  132.0 1.9 %copy-start.24 = (f32[160]{0:T(256)S(1)}, f32[160]{0:T(256)}, u32[]{:S(2)}) copy-start(f32[160]{0:T(256)} %param.33) | copy-start | bytes 1924
  133.9 4.6 %copy-start.1 = (bf16[3,3,320,320]{3,2,1,0:T(8,128)(2,1)S(1)}, bf16[3,3,320,320]{3,2,1,0:T(8,128)(2,1)}, u32[]{:S(2)}) copy-start(bf16[3,3,320,320]{3,2,1,0:T(8,128)(2,1)} %param.20) | copy-start | bytes 5529604
Sparse Core Ops, SparseCore 0:
  31.1 28.9 all-gather.2
  99.2 25.3 all-gather.4

commit v2 on v0

v2 whole, which is shorter than its diff:
```python
import functools

import jax
import jax.numpy as jnp
from jax import lax
from jax.experimental import pallas as pl
from jax.experimental.pallas import tpu as pltpu
from jax.sharding import PartitionSpec as P


groups = 32
norm_eps = 1e-05
side = 16
bf16 = jnp.bfloat16
f32 = jnp.float32
both = ("rows", "cols")


def call(kernel, out_shape, args, scratch=(), flops=0, outside=(), grant=24):
    return pl.pallas_call(
        kernel,
        out_shape=out_shape,
        in_specs=[pl.BlockSpec(memory_space=pl.ANY if at in outside else pltpu.VMEM) for at in range(len(args))],
        out_specs=jax.tree.map(lambda _: pl.BlockSpec(memory_space=pltpu.VMEM), out_shape),
        scratch_shapes=list(scratch),
        compiler_params=pltpu.CompilerParams(vmem_limit_bytes=grant * 1024 * 1024),
        cost_estimate=pl.CostEstimate(flops=flops, bytes_accessed=0, transcendentals=0),
    )(*args)


def shape(dims, kind=f32):
    return jax.ShapeDtypeStruct(dims, kind)


def exact_dot(left, right):
    return lax.dot_general(
        left, right, (((1,), (0,)), ((), ())), precision=lax.Precision.HIGHEST, preferred_element_type=f32
    )


def to_groups(chans, width, first, lane):
    chan = lax.broadcasted_iota(jnp.int32, (chans, 128), 0) + first
    low = (lax.broadcasted_iota(jnp.int32, (chans, 128), 1) - lane) * width
    return jnp.where((chan >= low) & (chan < low + width), 1.0, 0.0).astype(f32)


def from_groups(chan, width, lane):
    low = (lax.broadcasted_iota(jnp.int32, (128, chan.shape[1]), 0) - lane) * width
    return jnp.where((chan >= low) & (chan < low + width), 1.0, 0.0).astype(f32)


def group_row(sums, squares, width, first, lane):
    chans = sums.shape[1]
    row = exact_dot(jnp.broadcast_to(sums, (8, chans)), to_groups(chans, width, first, lane))
    row += exact_dot(jnp.broadcast_to(squares, (8, chans)), to_groups(chans, width, first, lane + groups))
    return row[0:1]


def statistics(total, count, width, lane, chan):
    total = jnp.broadcast_to(total, (8, 128)) / count
    mean = exact_dot(total, from_groups(chan, width, lane))[0:1]
    square = exact_dot(total, from_groups(chan, width, lane + groups))[0:1]
    return mean, lax.rsqrt(square - mean * mean + norm_eps)


def lane_ids(chans):
    return lax.broadcasted_iota(jnp.int32, (1, chans), 1)


def activate(value, mean, scale, shift):
    half = ((value - mean) * scale + shift) * 0.5
    return half + half * jnp.tanh(half)


def input_sums_kernel(widths, latent_ref, joined_ref, gain_ref, shift_ref, out_ref):
    def sums_of(ref):
        def step(row, carry):
            value = ref[row].astype(f32)
            return (
                carry[0] + jnp.sum(value, axis=0, keepdims=True),
                carry[1] + jnp.sum(value * value, axis=0, keepdims=True),
            )

        start = jnp.zeros((1, ref.shape[2]), f32)
        return lax.fori_loop(0, ref.shape[0], step, (start, start))

    row = group_row(*sums_of(latent_ref), widths[0], 0, 0)
    row += group_row(*sums_of(joined_ref), widths[1], 0, 2 * groups)
    count = out_ref.shape[0]
    shard = gain_ref.shape[1]
    room = (out_ref.shape[2] - 128) // 2
    out_ref[...] = jnp.zeros_like(out_ref)
    out_ref[:, :, 0:128] = jnp.broadcast_to(row[None], (count, 1, 128))
    out_ref[:, :, pl.ds(128, shard)] = jnp.broadcast_to(gain_ref[...][None], (count, 1, shard))
    out_ref[:, :, pl.ds(128 + room, shard)] = jnp.broadcast_to(shift_ref[...][None], (count, 1, shard))


def pack_level_one(weight_ref, packed_ref):
    chans = weight_ref.shape[2]
    for dy in range(3):
        for dx in range(3):
            packed_ref[pl.ds(dy * chans, chans), pl.ds(dx * chans, chans)] = weight_ref[dy, dx]


def store_taps(act_ref, block, value, blocks=None):
    chans = value.shape[1]
    for tap in range(3):
        if blocks is None or 0 <= block - tap < blocks:
            act_ref[block - tap, :, pl.ds(tap * chans, chans)] = value


def products(act_ref, packed_ref, prod_ref):
    blocks, wide, depth = act_ref.shape
    left = act_ref[...].reshape(blocks * wide, depth)
    prod_ref[pl.ds(8, blocks * wide), :] = jnp.dot(left, packed_ref[...], preferred_element_type=f32)


def shifted_sum(prod_ref, block, wide, keep):
    chans = prod_ref.shape[1] // 3
    rows = prod_ref[pl.ds(pl.multiple_of(block * wide, 8), wide + 16), :]
    return (
        rows[7 : 7 + keep, 0:chans]
        + rows[8 : 8 + keep, chans : 2 * chans]
        + rows[9 : 9 + keep, 2 * chans : 3 * chans]
    )


def edge_flags(sizes):
    row, col = lax.axis_index("rows"), lax.axis_index("cols")
    return row > 0, row < sizes[0] - 1, col > 0, col < sizes[1] - 1


def level_one_first_kernel(
    count, width, sizes, latent_ref, top_ref, low_ref, side_ref, sums_ref, gain_ref, shift_ref, weight_ref,
    hid_ref, row_ref, act_ref, packed_ref, prod_ref,
):
    rows, cols, chans = latent_ref.shape
    wide = cols + side
    has_top, has_low, has_left, has_right = edge_flags(sizes)
    total = jnp.sum(sums_ref[:, :, 0:128], axis=0)
    mean, inverse = statistics(total, count, width, 0, lane_ids(chans))
    scale, shift = inverse * gain_ref[...], shift_ref[...]
    pack_level_one(weight_ref, packed_ref)
    place = lax.broadcasted_iota(jnp.int32, (side, chans), 0)
    blocks = rows + 3

    def fill(block, main, main_ok, right_ok, left_ok, limit=None):
        edge = activate(side_ref[block].astype(f32), mean, scale, shift)
        keep = ((place < side // 2) & right_ok) | ((place >= side // 2) & left_ok)
        edge = jnp.where(keep, edge, 0.0)
        value = activate(main.astype(f32), mean, scale, shift)
        value = jnp.where(main_ok, value, 0.0)
        store_taps(act_ref, block, jnp.concatenate([value, edge], axis=0).astype(bf16), limit)

    never = has_top & jnp.logical_not(has_top)
    fill(0, latent_ref[0], never, never, has_left & has_top, blocks)
    fill(1, top_ref[0], has_top, has_right & has_top, has_left & has_top, blocks)
    fill(2, top_ref[1], has_top, has_right & has_top, has_left, blocks)

    def main_row(line, carry):
        fill(line + 3, latent_ref[line], True, has_right, has_left & ((line < rows - 1) | has_low))
        return carry

    lax.fori_loop(0, rows, main_row, 0)
    fill(rows + 3, low_ref[0], has_low, has_right & has_low, has_left & has_low, blocks)
    fill(rows + 4, low_ref[1], has_low, has_right & has_low, never, blocks)

    products(act_ref, packed_ref, prod_ref)

    def combine(block, carry):
        value = shifted_sum(prod_ref, block, wide, wide)
        hid_ref[block] = value
        main = value[0:cols]
        inner = jnp.where((block >= 2) & (block < rows + 2), 1.0, 0.0)
        main = main * inner
        return (
            carry[0] + jnp.sum(main, axis=0, keepdims=True),
            carry[1] + jnp.sum(main * main, axis=0, keepdims=True),
        )

    start = jnp.zeros((1, chans), f32)
    sums, squares = lax.fori_loop(0, blocks, combine, (start, start))
    row_ref[...] = group_row(sums, squares, width, 0, 0)


def level_one_second_kernel(
    count, width, sizes, hid_ref, latent_ref, sums_ref, gain_ref, shift_ref, weight_ref, bias_ref,
    out_ref, act_ref, packed_ref, prod_ref,
):
    rows, cols, chans = latent_ref.shape
    wide = cols + side
    has_top, has_low, has_left, has_right = edge_flags(sizes)
    total = jnp.sum(sums_ref[...], axis=0)
    mean, inverse = statistics(total, count, width, 0, lane_ids(chans))
    scale, shift = inverse * gain_ref[...], shift_ref[...]
    pack_level_one(weight_ref, packed_ref)
    place = lax.broadcasted_iota(jnp.int32, (wide, chans), 0)
    blocks = rows + 1

    def fill(block, main_ok, right_ok, left_ok, limit=None):
        value = activate(hid_ref[block], mean, scale, shift)
        keep = ((place < cols) & main_ok) | ((place == cols) & right_ok) | ((place == wide - 1) & left_ok)
        store_taps(act_ref, block, jnp.where(keep, value, 0.0).astype(bf16), limit)

    never = has_top & jnp.logical_not(has_top)
    fill(0, never, never, has_left & has_top, blocks)
    fill(1, has_top, has_right & has_top, has_left, blocks)

    def main_row(line, carry):
        fill(line + 2, True, has_right, has_left & ((line < rows - 1) | has_low))
        return carry

    lax.fori_loop(0, rows - 1, main_row, 0)
    fill(rows + 1, True, has_right, has_left & has_low, blocks)
    fill(rows + 2, has_low, has_right & has_low, never, blocks)

    products(act_ref, packed_ref, prod_ref)

    def combine(line, carry):
        value = shifted_sum(prod_ref, line + 1, wide, cols)
        out_ref[line] = (latent_ref[line].astype(f32) + value + bias_ref[...]).astype(bf16)
        return carry

    lax.fori_loop(0, rows, combine, 0)


def level_three_taps(left, right):
    dims = (((1,), (right[1],)), ((), ()))
    return lax.dot_general(left.reshape(-1, left.shape[2]), right[0], dims, preferred_element_type=f32)


def level_three_sum(prod_ref, line, cols, shard):
    lanes = pl.ds(line * cols, cols)
    place = lax.broadcasted_iota(jnp.int32, (shard, cols), 1)
    left = pltpu.roll(prod_ref[pl.ds(0, shard), lanes], 1, 1)
    right = pltpu.roll(prod_ref[pl.ds(2 * shard, shard), lanes], cols - 1, 1)
    left = jnp.where(place == 0, 0.0, left)
    right = jnp.where(place == cols - 1, 0.0, right)
    return left + prod_ref[pl.ds(shard, shard), lanes] + right


def level_three_first_kernel(
    count, width, sizes, near_ref, far_ref, near_edges_ref, far_edges_ref, sums_ref, gain_ref, shift_ref, weight_hbm, other_ref,
    hid_ref, local_ref, row_ref, act_ref, raw_ref, prod_ref, weight_ref, weight_sem,
):
    chips, height, tile, chans = near_ref.shape
    shard, cols = hid_ref.shape[1:]
    lines = height + 2
    fetch = pltpu.make_async_copy(weight_hbm, weight_ref, weight_sem)
    fetch.start()
    col_id = lax.axis_index("cols")
    has_top, has_low, _, _ = edge_flags(sizes)
    total = jnp.sum(sums_ref[:, :, 0:128], axis=0)
    mean, inverse = statistics(total, count, width, 2 * groups, lane_ids(chans))
    scale, shift = inverse * gain_ref[...], shift_ref[...]
    for hop in range(chips):
        for flip, (ref, edges) in enumerate(((near_ref, near_edges_ref), (far_ref, far_edges_ref))):
            place = pl.ds(pl.multiple_of((col_id ^ (2 * hop + flip)) * tile, tile), tile)

            def fill(line, carry):
                raw = ref[hop, line]
                raw_ref[line, place, :] = raw
                act_ref[line + 1, place, :] = activate(raw.astype(f32), mean, scale, shift).astype(bf16)
                return carry

            lax.fori_loop(0, height, fill, 0)
            for at, line, keep in ((0, 0, has_top), (1, lines - 1, has_low)):
                value = activate(edges[hop, at].astype(f32), mean, scale, shift)
                act_ref[line, place, :] = jnp.where(keep, value, 0.0).astype(bf16)

    chan = lax.broadcasted_iota(jnp.int32, (shard, chans), 1)
    wanted = lax.broadcasted_iota(jnp.int32, (shard, chans), 0) + col_id * shard
    pick = jnp.where(chan == wanted, 1.0, 0.0).astype(bf16)
    raw = raw_ref[...].reshape(height * cols, chans)
    local = level_three_taps(pick[None], (raw, 1)).astype(bf16)
    for line in range(height):
        local_ref[line] = local[:, line * cols : (line + 1) * cols]
    fetch.wait()
    total = None
    for dy in range(3):
        right = act_ref[pl.ds(dy, height)].reshape(height * cols, chans)
        part = level_three_taps(weight_ref[dy], (right, 1))
        total = part if total is None else total + part
    prod_ref[...] = total

    sums = squares = jnp.zeros((shard, cols), f32)
    for line in range(height):
        value = level_three_sum(prod_ref, line, cols, shard)
        hid_ref[line] = value.astype(bf16)
        sums, squares = sums + value, squares + value * value
    row = other_ref[...]
    for part, lane in ((sums, 2 * groups), (squares, 3 * groups)):
        column = jnp.sum(part, axis=1, keepdims=True)
        row += jnp.sum(column * to_groups(shard, width, col_id * shard, lane), axis=0, keepdims=True)
    row_ref[...] = jnp.broadcast_to(row[None], row_ref.shape)


def level_three_second_kernel(
    count, width, sizes, near_ref, far_ref, near_edges_ref, far_edges_ref, local_ref, sums_ref, affine_ref, weight_hbm, bias_ref,
    out_ref, act_ref, prod_ref, weight_ref, weight_sem,
):
    chips, height, shard, cols = near_ref.shape
    lines = height + 2
    fetch = pltpu.make_async_copy(weight_hbm, weight_ref, weight_sem)
    fetch.start()
    room = (affine_ref.shape[2] - 128) // 2
    row_id, col_id = lax.axis_index("rows"), lax.axis_index("cols")
    has_top, has_low, _, _ = edge_flags(sizes)
    total = jnp.sum(sums_ref[...], axis=0) / count
    first = row_id * sizes[1]
    place = lax.broadcasted_iota(jnp.int32, (shard, 128), 0)
    lane_at = lax.broadcasted_iota(jnp.int32, (shard, 128), 1)

    def column_of(row):
        found = jnp.zeros((shard, 128), f32)
        for start in range(0, room, 128):
            found += jnp.where(lane_at + start == place, row[:, start : start + 128], 0.0)
        return jnp.sum(found, axis=1, keepdims=True)

    for hop in range(chips):
        for flip, (ref, edges) in enumerate(((near_ref, near_edges_ref), (far_ref, far_edges_ref))):
            source = col_id ^ (2 * hop + flip)
            row = affine_ref[first + source]
            mean = jnp.sum(to_groups(shard, width, source * shard, 2 * groups) * total, axis=1, keepdims=True)
            square = jnp.sum(to_groups(shard, width, source * shard, 3 * groups) * total, axis=1, keepdims=True)
            scale = lax.rsqrt(square - mean * mean + norm_eps) * column_of(row[:, 128 : 128 + room])
            shift = column_of(row[:, 128 + room : 128 + 2 * room])
            chan = pl.ds(pl.multiple_of(source * shard, 16), shard)
            for line in range(lines):
                raw = edges[hop, min(line, 1)] if line in (0, lines - 1) else ref[hop, line - 1]
                value = activate(raw.astype(f32), mean, scale, shift)
                if line == 0:
                    value = jnp.where(has_top, value, 0.0)
                if line == lines - 1:
                    value = jnp.where(has_low, value, 0.0)
                act_ref[chan, pl.ds(line * cols, cols)] = value.astype(bf16)

    fetch.wait()
    total = None
    for dy in range(3):
        right = act_ref[:, pl.ds(dy * cols, height * cols)]
        part = level_three_taps(weight_ref[dy], (right, 0))
        total = part if total is None else total + part
    prod_ref[...] = total
    bias = column_of(bias_ref[...])
    for line in range(height):
        value = level_three_sum(prod_ref, line, cols, shard)
        out_ref[line] = (local_ref[line].astype(f32) + value + bias).astype(bf16)


def neighbours(low_edge, high_edge, axis):
    count = lax.axis_size(axis)
    forward = [(i, i + 1) for i in range(count - 1)]
    backward = [(target, source) for source, target in forward]
    return lax.ppermute(high_edge, axis, forward), lax.ppermute(low_edge, axis, backward)


def hop_to(value, step):
    return lax.ppermute(value, "cols", [(i, i ^ step) for i in range(lax.axis_size("cols"))])


def exchange(sent):
    return lax.all_to_all(sent, both, 0, 0)


def gathered(own, received, sums):
    *received, sums = lax.optimization_barrier((*received, sums))
    near = jnp.stack([own] + received)
    top, low = neighbours(near[:, 0:1], near[:, -1:], "rows")
    edges = jnp.concatenate([top, low], axis=1)
    return near, hop_to(near, 1), edges, hop_to(edges, 1), sums


def body(
    latent1, norm1a_g, norm1a_b, conv1a_w, norm1b_g, norm1b_b, conv1b_w, conv1b_b, feat3, adapter3,
    norm3a_g, norm3a_b, conv3a_w, norm3b_g, norm3b_b, conv3b_w, conv3b_b,
):
    sizes = (lax.axis_size("rows"), lax.axis_size("cols"))
    devices = sizes[0] * sizes[1]
    chips = sizes[1] // 2
    rows, cols, chans = latent1.shape
    wide = cols + side
    height, tile, deep = feat3.shape
    whole_cols = tile * sizes[1]
    shard = conv3a_w.shape[3]
    widths = (chans // groups, deep // groups)
    count_one = float(rows * cols * devices * widths[0])
    count_three = float(height * tile * devices * widths[1])
    row_of = lambda vector: vector.reshape(1, -1)

    top, low = neighbours(latent1[:2], latent1[-2:], "rows")
    joined = (feat3.astype(f32) + adapter3.astype(f32)).astype(bf16)
    edge = lambda at: jnp.concatenate([top[:, at], latent1[:, at], low[:, at]], axis=0)
    left, right = neighbours(edge(slice(0, 2)), edge(slice(cols - 2, cols)), "cols")
    beside = jnp.pad(right, ((1, 0), (0, side - 2), (0, 0))) + jnp.pad(left, ((0, 1), (side - 2, 0), (0, 0)))
    received = [hop_to(joined, 2 * k) for k in range(1, chips)]

    room = -(-shard // 128) * 128
    sent = call(
        functools.partial(input_sums_kernel, widths),
        shape((devices, 1, 128 + 2 * room)),
        (latent1, joined, row_of(norm3b_g), row_of(norm3b_b)),
    )
    sums = exchange(sent)
    near, far, near_edges, far_edges, sums = gathered(joined, received, sums)

    hid1, row_one = call(
        functools.partial(level_one_first_kernel, count_one, widths[0], sizes),
        (shape((rows + 3, wide, chans)), shape((1, 128))),
        (latent1, top, low, beside, sums, row_of(norm1a_g), row_of(norm1a_b), conv1a_w),
        (
            pltpu.VMEM((rows + 3, wide, 3 * chans), bf16),
            pltpu.VMEM((3 * chans, 3 * chans), bf16),
            pltpu.VMEM(((rows + 3) * wide + 16, 3 * chans), f32),
        ),
        flops=2 * rows * cols * 9 * chans * chans,
    )

    flops_three = 2 * height * whole_cols * 9 * deep * shard
    by_input = lambda weight: jnp.swapaxes(weight, 2, 3)
    tile_out = shape((height, shard, whole_cols), bf16)
    three_scratch = (
        pltpu.VMEM((3 * shard, height * whole_cols), f32),
        pltpu.VMEM((3, 3, shard, deep), bf16),
        pltpu.SemaphoreType.DMA,
    )
    hid3, local, sent_two = call(
        functools.partial(level_three_first_kernel, count_three, widths[1], sizes),
        (tile_out, tile_out, shape((devices, 1, 128))),
        (near, far, near_edges, far_edges, sums, row_of(norm3a_g), row_of(norm3a_b), by_input(conv3a_w), row_one),
        (pltpu.VMEM((height + 2, whole_cols, deep), bf16), pltpu.VMEM((height, whole_cols, deep), bf16)) + three_scratch,
        flops=flops_three,
        outside=(7,),
    )
    received = [hop_to(hid3, 2 * k) for k in range(1, chips)]
    sums_two = exchange(sent_two)
    near_two, far_two, near_edges_two, far_edges_two, sums_two = gathered(hid3, received, sums_two)

    out1 = call(
        functools.partial(level_one_second_kernel, count_one, widths[0], sizes),
        shape(latent1.shape, bf16),
        (hid1, latent1, sums_two, row_of(norm1b_g), row_of(norm1b_b), conv1b_w, row_of(conv1b_b)),
        (
            pltpu.VMEM((rows + 1, wide, 3 * chans), bf16),
            pltpu.VMEM((3 * chans, 3 * chans), bf16),
            pltpu.VMEM(((rows + 1) * wide + 16, 3 * chans), f32),
        ),
        flops=2 * rows * cols * 9 * chans * chans,
    )
    bias = jnp.pad(row_of(conv3b_b), ((0, 0), (0, room - shard)))
    out3 = call(
        functools.partial(level_three_second_kernel, count_three, widths[1], sizes),
        tile_out,
        (near_two, far_two, near_edges_two, far_edges_two, local, sums_two, sums, by_input(conv3b_w), bias),
        (pltpu.VMEM((deep, (height + 2) * whole_cols), bf16),) + three_scratch,
        flops=flops_three,
        outside=(7,),
    )
    return (out1, jnp.swapaxes(out3, 1, 2))


def solution(mesh):
    placed = (
        P("rows", "cols", None),
        P(),
        P(),
        P(),
        P(),
        P(),
        P(),
        P(),
        P("rows", "cols", None),
        P("rows", "cols", None),
        P(),
        P(),
        P(None, None, None, "cols"),
        P("cols"),
        P("cols"),
        P(None, None, None, "cols"),
        P("cols"),
    )
    return jax.shard_map(
        body,
        mesh=mesh,
        in_specs=placed,
        out_specs=(P("rows", "cols", None), P("rows", None, "cols")),
        check_vma=False,
    )
```

time: 273 us -> 116 us (0.42)
  the two profiles are of different devices: /device:TPU:4 before, /device:TPU:0 now
where the time goes in v2:
time: 116 us; the launch traced here: 115 us
  starting transfers between devices  34.4 us (30%)
  Pallas kernels  30 us (26%)
  waiting for transfers between devices  21.2 us (18%)
  blocking collectives  17.5 us (15%)
  local copies, waits for them, and re-layouts  7.29 us (6%)
  other arithmetic  3.28 us (3%)
  between operations  1.23 us (1%)
    pallas_call x5, Pallas kernels, call(): pl.pallas_call(kernel, out_shape=out_shape, in_specs=[pl.BlockSpec(memory...  30 us
    all_to_all x1, blocking collectives, exchange(): return lax.all_to_all(sent, both, 0, 0)  17.5 us
    ppermute x4, waiting for transfers between devices, neighbours(): lax.ppermute(low_edge, axis, backward)  13.5 us
    ppermute x10, starting transfers between devices, hop_to(): lax.ppermute(value, 'cols', [(i, i ^ step) for i in range(lax.axis_size('...  12.1 us
    ppermute x4, starting transfers between devices, neighbours(): lax.ppermute(high_edge, axis, forward)  10 us
    all_to_all x1, starting transfers between devices, exchange(): return lax.all_to_all(sent, both, 0, 0)  7 us
    all_to_all x1, waiting for transfers between devices, exchange(): return lax.all_to_all(sent, both, 0, 0)  5.93 us
    ppermute x4, starting transfers between devices, neighbours(): lax.ppermute(low_edge, axis, backward)  5.34 us
  transfers between devices with their start and end apart: 19, of which 5 were waited for; matrix products, arithmetic and copies ran while one was open for 6% of the time, Pallas kernels for 17%

profile of v2, /device:TPU:0, one launch (start us, length us, event | category | flops | bytes accessed | tf_op | source)
XLA Modules:
  0.0 114.9 jit_solution(14639378960372659481)
XLA Ops:
  0.6 0.0 copy-start.1
  0.6 1.1 add_convert_fusion.joined_ref
  1.8 0.0 copy-start.9
  1.8 3.1 %collective-permute-start.4 = (bf16[4,16,1280]{2,1,0:T(8,128)(2,1)S(1)}, bf16[4,16,1280]{2,1,0:T(8,128)(2,1)}, u32[]{:S(2)}, u32[]{:S(2)}) collective-permute-start(bf16[4,16,1280]{2,1,0:T(8,128)(2,1)S(1)} %add_convert_fusion.joined_ref), channel_id=1, source_target_pairs={{0,2},{1,3},{2,0},{3,1},{4,6},{5,7},{6,4},{7,5},{8,10},{9,11},{10,... | collective-permute-start | bytes 491528 | tf_op jit(solution)/shard_map/ppermute | solution.py:359
  4.9 2.6 %collective-permute-start.5 = (bf16[4,16,1280]{2,1,0:T(8,128)(2,1)S(1)}, bf16[4,16,1280]{2,1,0:T(8,128)(2,1)}, u32[]{:S(2)}, u32[]{:S(2)}) collective-permute-start(bf16[4,16,1280]{2,1,0:T(8,128)(2,1)S(1)} %add_convert_fusion.joined_ref), channel_id=1, source_target_pairs={{0,4},{1,5},{2,6},{3,7},{4,0},{5,1},{6,2},{7,3},{8,12},{9,13},{10,... | collective-permute-start | bytes 491528 | tf_op jit(solution)/shard_map/ppermute | solution.py:359
  7.5 0.0 collective-permute-start.6
  7.5 1.6 %fusion.1 = (bf16[2,64,320]{2,1,0:T(8,128)(2,1)}, bf16[2,64,320]{2,1,0:T(8,128)(2,1)S(1)}) fusion(bf16[16,64,320]{2,1,0:T(8,128)(2,1)} %latent_ref.5), kind=kLoop, calls=%fused_computation.11 | loop fusion | bytes 327680 | tf_op jit(solution)/shard_map/slice | solution.py:391
  9.1 3.6 %collective-permute-start = (bf16[2,64,320]{2,1,0:T(8,128)(2,1)S(1)}, bf16[2,64,320]{2,1,0:T(8,128)(2,1)S(1)}, u32[]{:S(2)}, u32[]{:S(2)}) collective-permute-start(bf16[2,64,320]{2,1,0:T(8,128)(2,1)S(1)} %get-tuple-element.31), channel_id=1, source_target_pairs={{0,8},{8,16},{16,24},{1,9},{9,17},{17,25},{2,10},{10,18},{18,26},{... | collective-permute-start | bytes 245768 | tf_op jit(solution)/shard_map/ppermute | solution.py:355
  12.7 1.3 %collective-permute-start.1 = (bf16[2,64,320]{2,1,0:T(8,128)(2,1)}, bf16[2,64,320]{2,1,0:T(8,128)(2,1)S(1)}, u32[]{:S(2)}, u32[]{:S(2)}) collective-permute-start(bf16[2,64,320]{2,1,0:T(8,128)(2,1)} %get-tuple-element.30), channel_id=1, source_target_pairs={{8,0},{16,8},{24,16},{9,1},{17,9},{25,17},{10,2},{18,10},{26,18},{... | collective-permute-start | bytes 245768 | tf_op jit(solution)/shard_map/ppermute | solution.py:355
  14.0 0.0 copy-start
  14.0 1.1 copy-done
  15.1 0.7 copy-done.2
  15.8 0.7 copy-done.3
  16.5 2.4 %shard_map.176 = f32[32,1,640]{2,1,0:T(1,128)} custom-call(bf16[16,64,320]{2,1,0:T(8,128)(2,1)S(1)} %copy-done, bf16[4,16,1280]{2,1,0:T(8,128)(2,1)S(1)} %add_convert_fusion.joined_ref, f32[1,160]{1,0:T(1,128)S(1)} %bitcast.16, f32[1,160]{1,0:T(1,128)S(1)} %bitcast.17), custom_call_target="tpu_custom_call" | custom-call | tf_op jit(solution)/shard_map/pallas_call | solution.py:20
  18.9 7.0 %all-to-all-start = ((f32[32,1,640]{2,1,0:T(1,128)}), f32[32,1,640]{2,1,0:T(1,128)S(1)}, u32[]{:S(2)}, u32[]{:S(2)}) async-start(f32[32,1,640]{2,1,0:T(1,128)} %shard_map.176), calls=%async_computation | async-start | bytes 163840 | tf_op jit(solution)/shard_map/all_to_all | solution.py:363
  25.9 1.6 %fusion = (bf16[16,2,320]{2,1,0:T(2,128)(2,1)}, bf16[16,2,320]{2,1,0:T(2,128)(2,1)}) fusion(bf16[16,64,320]{2,1,0:T(8,128)(2,1)} %latent_ref.5), kind=kLoop, calls=%fused_computation.10 | loop fusion | bytes 81920 | tf_op jit(solution)/shard_map/slice | solution.py:393
  27.5 0.0 collective-permute-done.1.low_ref
  27.5 5.9 %all-to-all-done.sums_ref.affine_ref = f32[32,1,640]{2,1,0:T(1,128)S(1)} async-done(((f32[32,1,640]{2,1,0:T(1,128)}), f32[32,1,640]{2,1,0:T(1,128)S(1)}, u32[]{:S(2)}, u32[]{:S(2)}) %all-to-all-start) | async-done | bytes 81952 | tf_op jit(solution)/shard_map/all_to_all | solution.py:363
  33.4 0.0 collective-permute-done.4
  33.4 0.0 collective-permute-done.5
  33.4 0.0 collective-permute-done.6
  33.5 1.2 %pad_maximum_fusion.near_ref = bf16[4,4,16,1280]{3,2,1,0:T(8,128)(2,1)S(1)} fusion(bf16[1,4,16,1280]{3,2,1,0:T(8,128)(2,1)} %bitcast.5, bf16[1,4,16,1280]{3,2,1,0:T(8,128)(2,1)} %bitcast.4, bf16[1,4,16,1280]{3,2,1,0:T(8,128)(2,1)} %bitcast.3, bf16[1,4,16,1280]{3,2,1,0:T(8,128)(2,1)S(1)} %bitcast.14), kind=kLoop, calls=%fused_computation | loop fusion | flops 983040 | bytes 1310720 | tf_op jit(solution)/shard_map/stack | solution.py:368
  34.7 2.6 %collective-permute-start.8 = (bf16[4,1,16,1280]{3,2,1,0:T(8,128)(2,1)S(1)}, bf16[4,1,16,1280]{3,2,1,0:T(8,128)(2,1)S(1)}, u32[]{:S(2)}, u32[]{:S(2)}) collective-permute-start(bf16[4,1,16,1280]{3,2,1,0:T(8,128)(2,1)S(1)} %get-tuple-element.35), channel_id=1, source_target_pairs={{0,8},{8,16},{16,24},{1,9},{9,17},{17,25},{2,10},{10,18},{18,26},{... | collective-permute-start | bytes 491528 | tf_op jit(solution)/shard_map/ppermute | solution.py:355
  37.3 0.0 collective-permute-done.top_ref
  37.3 0.8 pad_maximum_fusion.3
  38.1 1.3 %collective-permute-start.3 = (bf16[20,2,320]{2,1,0:T(2,128)(2,1)S(1)}, bf16[20,2,320]{2,1,0:T(2,128)(2,1)S(1)}, u32[]{:S(2)}, u32[]{:S(2)}) collective-permute-start(bf16[20,2,320]{2,1,0:T(2,128)(2,1)S(1)} %pad_maximum_fusion.3), channel_id=1, source_target_pairs={{0,1},{1,2},{2,3},{3,4},{4,5},{5,6},{6,7},{8,9},{9,10},{10,11},{11... | collective-permute-start | bytes 76808 | tf_op jit(solution)/shard_map/ppermute | solution.py:355
  39.4 1.2 %collective-permute-start.7 = (bf16[4,4,16,1280]{3,2,1,0:T(8,128)(2,1)S(1)}, bf16[4,4,16,1280]{3,2,1,0:T(8,128)(2,1)S(1)}, u32[]{:S(2)}, u32[]{:S(2)}) collective-permute-start(bf16[4,4,16,1280]{3,2,1,0:T(8,128)(2,1)S(1)} %pad_maximum_fusion.near_ref), channel_id=1, source_target_pairs={{0,1},{1,0},{2,3},{3,2},{4,5},{5,4},{6,7},{7,6},{8,9},{9,8},{10,11... | collective-permute-start | bytes 1966088 | tf_op jit(solution)/shard_map/ppermute | solution.py:359
  40.6 1.3 %collective-permute-start.9 = (bf16[4,1,16,1280]{3,2,1,0:T(8,128)(2,1)S(1)}, bf16[4,1,16,1280]{3,2,1,0:T(8,128)(2,1)S(1)}, u32[]{:S(2)}, u32[]{:S(2)}) collective-permute-start(bf16[4,1,16,1280]{3,2,1,0:T(8,128)(2,1)S(1)} %get-tuple-element.34), channel_id=1, source_target_pairs={{8,0},{16,8},{24,16},{9,1},{17,9},{25,17},{10,2},{18,10},{26,18},{... | collective-permute-start | bytes 491528 | tf_op jit(solution)/shard_map/ppermute | solution.py:355
  41.9 0.0 collective-permute-done.8
  41.9 6.7 %collective-permute-done.9 = bf16[4,1,16,1280]{3,2,1,0:T(8,128)(2,1)S(1)} collective-permute-done((bf16[4,1,16,1280]{3,2,1,0:T(8,128)(2,1)S(1)}, bf16[4,1,16,1280]{3,2,1,0:T(8,128)(2,1)S(1)}, u32[]{:S(2)}, u32[]{:S(2)}) %collective-permute-start.9) | collective-permute-done | bytes 163872 | tf_op jit(solution)/shard_map/ppermute | solution.py:355
  48.6 0.1 collective-permute-start.10
  48.7 0.1 pad_maximum_fusion.2
  48.8 1.3 %collective-permute-start.2 = (bf16[20,2,320]{2,1,0:T(2,128)(2,1)S(1)}, bf16[20,2,320]{2,1,0:T(2,128)(2,1)S(1)}, u32[]{:S(2)}, u32[]{:S(2)}) collective-permute-start(bf16[20,2,320]{2,1,0:T(2,128)(2,1)S(1)} %pad_maximum_fusion.2), channel_id=1, source_target_pairs={{1,0},{2,1},{3,2},{4,3},{5,4},{6,5},{7,6},{9,8},{10,9},{11,10},{12... | collective-permute-start | bytes 76808 | tf_op jit(solution)/shard_map/ppermute | solution.py:355
  50.1 0.7 reshape.36.gain_ref
  50.8 0.7 reshape.37.shift_ref
  51.5 0.4 collective-permute-done.2
  51.9 0.1 pad_add_fusion.side_ref
  52.0 0.0 copy-start.4
  52.0 9.0 %shard_map.177 = (f32[19,80,320]{2,1,0:T(8,128)S(1)}, f32[1,128]{1,0:T(1,128)S(1)}) custom-call(bf16[16,64,320]{2,1,0:T(8,128)(2,1)S(1)} %copy-done.1, bf16[2,64,320]{2,1,0:T(8,128)(2,1)S(1)} %collective-permute-done.top_ref, bf16[2,64,320]{2,1,0:T(8,128)(2,1)S(1)} %collective-permute-done.1.low_ref, bf16[21,16,320]{2,1,0:T(8,128)(2,1)S(1)} %pad_add_fusion.side_ref, ...), custom_call_target="tpu_custom_call" | custom-call | flops 1887436800 | tf_op jit(solution)/shard_map/pallas_call | solution.py:20
  61.0 0.0 collective-permute-done.10.far_edges_ref
  61.0 0.0 collective-permute-done.7.far_ref
  61.0 0.0 copy-done.4
  61.0 5.6 %shard_map.178 = (bf16[4,160,128]{2,1,0:T(8,128)(2,1)S(1)}, bf16[4,160,128]{2,1,0:T(8,128)(2,1)S(1)}, f32[32,1,128]{2,1,0:T(1,128)S(1)}) custom-call(bf16[4,4,16,1280]{3,2,1,0:T(8,128)(2,1)S(1)} %pad_maximum_fusion.near_ref, bf16[4,4,16,1280]{3,2,1,0:T(8,128)(2,1)S(1)} %collective-permute-done.7.far_ref, ...), custom_call_target="tpu_custom_call" | custom-call | flops 1887436800 | tf_op jit(solution)/shard_map/pallas_call | solution.py:20
  66.6 0.0 copy-start.11
  66.6 0.0 copy-start.12
  66.6 0.0 copy-start.13
  66.7 0.0 copy-start.14
  66.7 0.0 copy-start.7
  66.7 2.6 %collective-permute-start.11 = (bf16[4,160,128]{2,1,0:T(8,128)(2,1)S(1)}, bf16[4,160,128]{2,1,0:T(8,128)(2,1)S(1)}, u32[]{:S(2)}, u32[]{:S(2)}) collective-permute-start(bf16[4,160,128]{2,1,0:T(8,128)(2,1)S(1)} %get-tuple-element.21), channel_id=1, source_target_pairs={{0,2},{1,3},{2,0},{3,1},{4,6},{5,7},{6,4},{7,5},{8,10},{9,11},{10,... | collective-permute-start | bytes 491528 | tf_op jit(solution)/shard_map/ppermute | solution.py:359
  69.2 1.0 collective-permute-start.12
  70.3 1.4 %collective-permute-start.13 = (bf16[4,160,128]{2,1,0:T(8,128)(2,1)S(1)}, bf16[4,160,128]{2,1,0:T(8,128)(2,1)S(1)}, u32[]{:S(2)}, u32[]{:S(2)}) collective-permute-start(bf16[4,160,128]{2,1,0:T(8,128)(2,1)S(1)} %get-tuple-element.21), channel_id=1, source_target_pairs={{0,6},{1,7},{2,4},{3,5},{4,2},{5,3},{6,0},{7,1},{8,14},{9,15},{10,... | collective-permute-start | bytes 491528 | tf_op jit(solution)/shard_map/ppermute | solution.py:359
  71.7 17.5 %all_to_all.10.sums_ref = f32[32,1,128]{2,1,0:T(1,128)S(1)} all-to-all(f32[32,1,128]{2,1,0:T(1,128)S(1)} %get-tuple-element.22), channel_id=1, replica_groups=mesh['rows'=4,'cols'=8] {'rows','cols'}, dimensions={0} | all-to-all | bytes 32768 | tf_op jit(solution)/shard_map/all_to_all | solution.py:363
  89.2 0.0 collective-permute-done.11
  89.2 0.0 collective-permute-done.12
  89.2 0.1 pad_maximum_fusion.1.near_ref
  89.3 2.5 %collective-permute-start.15 = (bf16[4,1,160,128]{3,2,1,0:T(8,128)(2,1)S(1)}, bf16[4,1,160,128]{3,2,1,0:T(8,128)(2,1)S(1)}, u32[]{:S(2)}, u32[]{:S(2)}) collective-permute-start(bf16[4,1,160,128]{3,2,1,0:T(8,128)(2,1)S(1)} %get-tuple-element.33), channel_id=1, source_target_pairs={{0,8},{8,16},{16,24},{1,9},{9,17},{17,25},{2,10},{10,18},{18,26},{... | collective-permute-start | bytes 491528 | tf_op jit(solution)/shard_map/ppermute | solution.py:355
  91.8 0.1 collective-permute-start.14
  91.9 1.5 %collective-permute-start.16 = (bf16[4,1,160,128]{3,2,1,0:T(8,128)(2,1)S(1)}, bf16[4,1,160,128]{3,2,1,0:T(8,128)(2,1)S(1)}, u32[]{:S(2)}, u32[]{:S(2)}) collective-permute-start(bf16[4,1,160,128]{3,2,1,0:T(8,128)(2,1)S(1)} %get-tuple-element.32), channel_id=1, source_target_pairs={{8,0},{16,8},{24,16},{9,1},{17,9},{25,17},{10,2},{18,10},{26,18},{... | collective-permute-start | bytes 491528 | tf_op jit(solution)/shard_map/ppermute | solution.py:355
  93.4 1.8 %collective-permute-done.15 = bf16[4,1,160,128]{3,2,1,0:T(8,128)(2,1)S(1)} collective-permute-done((bf16[4,1,160,128]{3,2,1,0:T(8,128)(2,1)S(1)}, bf16[4,1,160,128]{3,2,1,0:T(8,128)(2,1)S(1)}, u32[]{:S(2)}, u32[]{:S(2)}) %collective-permute-start.15) | collective-permute-done | bytes 163872 | tf_op jit(solution)/shard_map/ppermute | solution.py:355
  95.2 6.4 %collective-permute-done.16 = bf16[4,1,160,128]{3,2,1,0:T(8,128)(2,1)S(1)} collective-permute-done((bf16[4,1,160,128]{3,2,1,0:T(8,128)(2,1)S(1)}, bf16[4,1,160,128]{3,2,1,0:T(8,128)(2,1)S(1)}, u32[]{:S(2)}, u32[]{:S(2)}) %collective-permute-start.16) | collective-permute-done | bytes 163872 | tf_op jit(solution)/shard_map/ppermute | solution.py:355
  101.6 0.1 collective-permute-start.17
  101.8 0.0 copy-start.5
  101.8 8.0 %shard_map.179 = bf16[16,64,320]{2,1,0:T(8,128)(2,1)} custom-call(f32[19,80,320]{2,1,0:T(8,128)S(1)} %get-tuple-element.16.hid_ref, bf16[16,64,320]{2,1,0:T(8,128)(2,1)S(1)} %copy-done.1, f32[32,1,128]{2,1,0:T(1,128)S(1)} %all_to_all.10.sums_ref, f32[1,320]{1,0:T(1,128)S(1)} %reshape.40.gain_ref, f32[1,320]{1,0:T(1,128)S(1)} %reshape.41.shift_ref, ...), custom_call_target="tpu_custom_call" | custom-call | flops 1887436800 | tf_op jit(solution)/shard_map/pallas_call | solution.py:20
  109.8 4.9 %shard_map.180 = bf16[4,160,128]{2,1,0:T(8,128)(2,1)} custom-call(bf16[4,4,160,128]{3,2,1,0:T(8,128)(2,1)S(1)} %pad_maximum_fusion.1.near_ref, bf16[4,4,160,128]{3,2,1,0:T(8,128)(2,1)S(1)} %collective-permute-done.14.far_ref, bf16[4,2,160,128]{3,2,1,0:T(8,128)(2,1)S(1)} %constant_dynamic-update-slice_fusion.2.near_edges_ref, ...), custom_call_target="tpu_custom_call" | custom-call | flops 1887436800 | tf_op jit(solution)/shard_map/pallas_call | solution.py:20
  (34 shorter events, 0.2 us)
Async XLA Ops:
  0.6 51.3 %copy-start.1 = (bf16[16,64,320]{2,1,0:T(8,128)(2,1)S(1)}, bf16[16,64,320]{2,1,0:T(8,128)(2,1)}, u32[]{:S(2)}) copy-start(bf16[16,64,320]{2,1,0:T(8,128)(2,1)} %latent_ref.5) | copy-start | bytes 1966084
  1.8 49.7 %copy-start.9 = (f32[1280]{0:T(1024)S(1)}, f32[1280]{0:T(1024)}, u32[]{:S(2)}) copy-start(f32[1280]{0:T(1024)} %param.27) | copy-start | bytes 15364
  1.8 31.7 %collective-permute-start.4 = (bf16[4,16,1280]{2,1,0:T(8,128)(2,1)S(1)}, bf16[4,16,1280]{2,1,0:T(8,128)(2,1)}, u32[]{:S(2)}, u32[]{:S(2)}) collective-permute-start(bf16[4,16,1280]{2,1,0:T(8,128)(2,1)S(1)} %add_convert_fusion.joined_ref), channel_id=1, source_target_pairs={{0,2},{1,3},{2,0},{3,1},{4,6},{5,7},{6,4},{7,5},{8,10},{9,11},{10,... | collective-permute-start | bytes 491528 | tf_op jit(solution)/shard_map/ppermute | solution.py:359
  4.9 28.6 %collective-permute-start.5 = (bf16[4,16,1280]{2,1,0:T(8,128)(2,1)S(1)}, bf16[4,16,1280]{2,1,0:T(8,128)(2,1)}, u32[]{:S(2)}, u32[]{:S(2)}) collective-permute-start(bf16[4,16,1280]{2,1,0:T(8,128)(2,1)S(1)} %add_convert_fusion.joined_ref), channel_id=1, source_target_pairs={{0,4},{1,5},{2,6},{3,7},{4,0},{5,1},{6,2},{7,3},{8,12},{9,13},{10,... | collective-permute-start | bytes 491528 | tf_op jit(solution)/shard_map/ppermute | solution.py:359
  7.5 26.0 %collective-permute-start.6 = (bf16[4,16,1280]{2,1,0:T(8,128)(2,1)S(1)}, bf16[4,16,1280]{2,1,0:T(8,128)(2,1)}, u32[]{:S(2)}, u32[]{:S(2)}) collective-permute-start(bf16[4,16,1280]{2,1,0:T(8,128)(2,1)S(1)} %add_convert_fusion.joined_ref), channel_id=1, source_target_pairs={{0,6},{1,7},{2,4},{3,5},{4,2},{5,3},{6,0},{7,1},{8,14},{9,15},{10,... | collective-permute-start | bytes 491528 | tf_op jit(solution)/shard_map/ppermute | solution.py:359
  9.1 28.2 %collective-permute-start = (bf16[2,64,320]{2,1,0:T(8,128)(2,1)S(1)}, bf16[2,64,320]{2,1,0:T(8,128)(2,1)S(1)}, u32[]{:S(2)}, u32[]{:S(2)}) collective-permute-start(bf16[2,64,320]{2,1,0:T(8,128)(2,1)S(1)} %get-tuple-element.31), channel_id=1, source_target_pairs={{0,8},{8,16},{16,24},{1,9},{9,17},{17,25},{2,10},{10,18},{18,26},{... | collective-permute-start | bytes 245768 | tf_op jit(solution)/shard_map/ppermute | solution.py:355
  12.7 14.8 %collective-permute-start.1 = (bf16[2,64,320]{2,1,0:T(8,128)(2,1)}, bf16[2,64,320]{2,1,0:T(8,128)(2,1)S(1)}, u32[]{:S(2)}, u32[]{:S(2)}) collective-permute-start(bf16[2,64,320]{2,1,0:T(8,128)(2,1)} %get-tuple-element.30), channel_id=1, source_target_pairs={{8,0},{16,8},{24,16},{9,1},{17,9},{25,17},{10,2},{18,10},{26,18},{... | collective-permute-start | bytes 245768 | tf_op jit(solution)/shard_map/ppermute | solution.py:355
  14.0 1.1 copy-start
  15.1 0.7 copy-start.2
  15.8 0.7 copy-start.3
  16.5 35.5 %copy-start.6 = (bf16[3,3,320,320]{3,2,1,0:T(8,128)(2,1)S(1)}, bf16[3,3,320,320]{3,2,1,0:T(8,128)(2,1)}, u32[]{:S(2)}) copy-start(bf16[3,3,320,320]{3,2,1,0:T(8,128)(2,1)} %weight_ref.2) | copy-start | bytes 5529604
  18.9 14.6 %all-to-all-start = ((f32[32,1,640]{2,1,0:T(1,128)}), f32[32,1,640]{2,1,0:T(1,128)S(1)}, u32[]{:S(2)}, u32[]{:S(2)}) async-start(f32[32,1,640]{2,1,0:T(1,128)} %shard_map.176), calls=%async_computation | async-start | bytes 163840 | tf_op jit(solution)/shard_map/all_to_all | solution.py:363
  33.4 15.3 %copy-start.8 = (bf16[16,2,320]{2,1,0:T(2,128)(2,1)S(1)}, bf16[16,2,320]{2,1,0:T(2,128)(2,1)}, u32[]{:S(2)}) copy-start(bf16[16,2,320]{2,1,0:T(2,128)(2,1)} %get-tuple-element.28) | copy-start | bytes 61444
  33.4 18.0 %copy-start.10 = (f32[1280]{0:T(1024)S(1)}, f32[1280]{0:T(1024)}, u32[]{:S(2)}) copy-start(f32[1280]{0:T(1024)} %param.28) | copy-start | bytes 15364
  34.7 7.2 %collective-permute-start.8 = (bf16[4,1,16,1280]{3,2,1,0:T(8,128)(2,1)S(1)}, bf16[4,1,16,1280]{3,2,1,0:T(8,128)(2,1)S(1)}, u32[]{:S(2)}, u32[]{:S(2)}) collective-permute-start(bf16[4,1,16,1280]{3,2,1,0:T(8,128)(2,1)S(1)} %get-tuple-element.35), channel_id=1, source_target_pairs={{0,8},{8,16},{16,24},{1,9},{9,17},{17,25},{2,10},{10,18},{18,26},{... | collective-permute-start | bytes 491528 | tf_op jit(solution)/shard_map/ppermute | solution.py:355
  38.1 13.4 %collective-permute-start.3 = (bf16[20,2,320]{2,1,0:T(2,128)(2,1)S(1)}, bf16[20,2,320]{2,1,0:T(2,128)(2,1)S(1)}, u32[]{:S(2)}, u32[]{:S(2)}) collective-permute-start(bf16[20,2,320]{2,1,0:T(2,128)(2,1)S(1)} %pad_maximum_fusion.3), channel_id=1, source_target_pairs={{0,1},{1,2},{2,3},{3,4},{4,5},{5,6},{6,7},{8,9},{9,10},{10,11},{11... | collective-permute-start | bytes 76808 | tf_op jit(solution)/shard_map/ppermute | solution.py:355
  39.4 21.6 %collective-permute-start.7 = (bf16[4,4,16,1280]{3,2,1,0:T(8,128)(2,1)S(1)}, bf16[4,4,16,1280]{3,2,1,0:T(8,128)(2,1)S(1)}, u32[]{:S(2)}, u32[]{:S(2)}) collective-permute-start(bf16[4,4,16,1280]{3,2,1,0:T(8,128)(2,1)S(1)} %pad_maximum_fusion.near_ref), channel_id=1, source_target_pairs={{0,1},{1,0},{2,3},{3,2},{4,5},{5,4},{6,7},{7,6},{8,9},{9,8},{10,11... | collective-permute-start | bytes 1966088 | tf_op jit(solution)/shard_map/ppermute | solution.py:359
  40.6 8.0 %collective-permute-start.9 = (bf16[4,1,16,1280]{3,2,1,0:T(8,128)(2,1)S(1)}, bf16[4,1,16,1280]{3,2,1,0:T(8,128)(2,1)S(1)}, u32[]{:S(2)}, u32[]{:S(2)}) collective-permute-start(bf16[4,1,16,1280]{3,2,1,0:T(8,128)(2,1)S(1)} %get-tuple-element.34), channel_id=1, source_target_pairs={{8,0},{16,8},{24,16},{9,1},{17,9},{25,17},{10,2},{18,10},{26,18},{... | collective-permute-start | bytes 491528 | tf_op jit(solution)/shard_map/ppermute | solution.py:355
  48.6 12.4 %collective-permute-start.10 = (bf16[4,2,16,1280]{3,2,1,0:T(8,128)(2,1)S(1)}, bf16[4,2,16,1280]{3,2,1,0:T(8,128)(2,1)S(1)}, u32[]{:S(2)}, u32[]{:S(2)}) collective-permute-start(bf16[4,2,16,1280]{3,2,1,0:T(8,128)(2,1)S(1)} %constant_dynamic-update-slice_fusion.near_edges_ref), channel_id=1, source_target_pairs={{0,1},{1,0},{2,3},{3,2},{4,5},{5,4},{6,7},{7,6},{8,9},{9,8},{10,11... | collective-permute-start | bytes 983048 | tf_op jit(solution)/shard_map/ppermute | solution.py:359
  48.8 3.1 %collective-permute-start.2 = (bf16[20,2,320]{2,1,0:T(2,128)(2,1)S(1)}, bf16[20,2,320]{2,1,0:T(2,128)(2,1)S(1)}, u32[]{:S(2)}, u32[]{:S(2)}) collective-permute-start(bf16[20,2,320]{2,1,0:T(2,128)(2,1)S(1)} %pad_maximum_fusion.2), channel_id=1, source_target_pairs={{1,0},{2,1},{3,2},{4,3},{5,4},{6,5},{7,6},{9,8},{10,9},{11,10},{12... | collective-permute-start | bytes 76808 | tf_op jit(solution)/shard_map/ppermute | solution.py:355
  52.0 9.0 %copy-start.4 = (bf16[3,3,1280,160]{2,3,1,0:T(8,128)(2,1)S(1)}, bf16[3,3,1280,160]{2,3,1,0:T(8,128)(2,1)}, u32[]{:S(2)}) copy-start(bf16[3,3,1280,160]{2,3,1,0:T(8,128)(2,1)} %param.29) | copy-start | bytes 11059204
  66.6 35.1 %copy-start.11 = (f32[320]{0:T(512)S(1)}, f32[320]{0:T(512)}, u32[]{:S(2)}) copy-start(f32[320]{0:T(512)} %param.21) | copy-start | bytes 3844
  66.6 35.1 %copy-start.12 = (f32[320]{0:T(512)S(1)}, f32[320]{0:T(512)}, u32[]{:S(2)}) copy-start(f32[320]{0:T(512)} %param.22) | copy-start | bytes 3844
  66.6 35.1 %copy-start.13 = (f32[320]{0:T(512)S(1)}, f32[320]{0:T(512)}, u32[]{:S(2)}) copy-start(f32[320]{0:T(512)} %param.24) | copy-start | bytes 3844
  66.7 35.1 %copy-start.14 = (f32[160]{0:T(256)S(1)}, f32[160]{0:T(256)}, u32[]{:S(2)}) copy-start(f32[160]{0:T(256)} %param.33) | copy-start | bytes 1924
  66.7 35.1 %copy-start.7 = (bf16[3,3,320,320]{3,2,1,0:T(8,128)(2,1)S(1)}, bf16[3,3,320,320]{3,2,1,0:T(8,128)(2,1)}, u32[]{:S(2)}) copy-start(bf16[3,3,320,320]{3,2,1,0:T(8,128)(2,1)} %weight_ref.3) | copy-start | bytes 5529604
  66.7 22.5 %collective-permute-start.11 = (bf16[4,160,128]{2,1,0:T(8,128)(2,1)S(1)}, bf16[4,160,128]{2,1,0:T(8,128)(2,1)S(1)}, u32[]{:S(2)}, u32[]{:S(2)}) collective-permute-start(bf16[4,160,128]{2,1,0:T(8,128)(2,1)S(1)} %get-tuple-element.21), channel_id=1, source_target_pairs={{0,2},{1,3},{2,0},{3,1},{4,6},{5,7},{6,4},{7,5},{8,10},{9,11},{10,... | collective-permute-start | bytes 491528 | tf_op jit(solution)/shard_map/ppermute | solution.py:359
  69.2 20.0 %collective-permute-start.12 = (bf16[4,160,128]{2,1,0:T(8,128)(2,1)S(1)}, bf16[4,160,128]{2,1,0:T(8,128)(2,1)S(1)}, u32[]{:S(2)}, u32[]{:S(2)}) collective-permute-start(bf16[4,160,128]{2,1,0:T(8,128)(2,1)S(1)} %get-tuple-element.21), channel_id=1, source_target_pairs={{0,4},{1,5},{2,6},{3,7},{4,0},{5,1},{6,2},{7,3},{8,12},{9,13},{10,... | collective-permute-start | bytes 491528 | tf_op jit(solution)/shard_map/ppermute | solution.py:359
  70.3 18.9 %collective-permute-start.13 = (bf16[4,160,128]{2,1,0:T(8,128)(2,1)S(1)}, bf16[4,160,128]{2,1,0:T(8,128)(2,1)S(1)}, u32[]{:S(2)}, u32[]{:S(2)}) collective-permute-start(bf16[4,160,128]{2,1,0:T(8,128)(2,1)S(1)} %get-tuple-element.21), channel_id=1, source_target_pairs={{0,6},{1,7},{2,4},{3,5},{4,2},{5,3},{6,0},{7,1},{8,14},{9,15},{10,... | collective-permute-start | bytes 491528 | tf_op jit(solution)/shard_map/ppermute | solution.py:359
  89.3 5.9 %collective-permute-start.15 = (bf16[4,1,160,128]{3,2,1,0:T(8,128)(2,1)S(1)}, bf16[4,1,160,128]{3,2,1,0:T(8,128)(2,1)S(1)}, u32[]{:S(2)}, u32[]{:S(2)}) collective-permute-start(bf16[4,1,160,128]{3,2,1,0:T(8,128)(2,1)S(1)} %get-tuple-element.33), channel_id=1, source_target_pairs={{0,8},{8,16},{16,24},{1,9},{9,17},{17,25},{2,10},{10,18},{18,26},{... | collective-permute-start | bytes 491528 | tf_op jit(solution)/shard_map/ppermute | solution.py:355
  91.8 18.0 %collective-permute-start.14 = (bf16[4,4,160,128]{3,2,1,0:T(8,128)(2,1)S(1)}, bf16[4,4,160,128]{3,2,1,0:T(8,128)(2,1)S(1)}, u32[]{:S(2)}, u32[]{:S(2)}) collective-permute-start(bf16[4,4,160,128]{3,2,1,0:T(8,128)(2,1)S(1)} %pad_maximum_fusion.1.near_ref), channel_id=1, source_target_pairs={{0,1},{1,0},{2,3},{3,2},{4,5},{5,4},{6,7},{7,6},{8,9},{9,8},{10,11... | collective-permute-start | bytes 1966088 | tf_op jit(solution)/shard_map/ppermute | solution.py:359
  91.9 9.7 %collective-permute-start.16 = (bf16[4,1,160,128]{3,2,1,0:T(8,128)(2,1)S(1)}, bf16[4,1,160,128]{3,2,1,0:T(8,128)(2,1)S(1)}, u32[]{:S(2)}, u32[]{:S(2)}) collective-permute-start(bf16[4,1,160,128]{3,2,1,0:T(8,128)(2,1)S(1)} %get-tuple-element.32), channel_id=1, source_target_pairs={{8,0},{16,8},{24,16},{9,1},{17,9},{25,17},{10,2},{18,10},{26,18},{... | collective-permute-start | bytes 491528 | tf_op jit(solution)/shard_map/ppermute | solution.py:355
  101.6 8.2 %collective-permute-start.17 = (bf16[4,2,160,128]{3,2,1,0:T(8,128)(2,1)S(1)}, bf16[4,2,160,128]{3,2,1,0:T(8,128)(2,1)S(1)}, u32[]{:S(2)}, u32[]{:S(2)}) collective-permute-start(bf16[4,2,160,128]{3,2,1,0:T(8,128)(2,1)S(1)} %constant_dynamic-update-slice_fusion.2.near_edges_ref), channel_id=1, source_target_pairs={{0,1},{1,0},{2,3},{3,2},{4,5},{5,4},{6,7},{7,6},{8,9},{9,8},{10,11... | collective-permute-start | bytes 983048 | tf_op jit(solution)/shard_map/ppermute | solution.py:359
  101.8 8.0 %copy-start.5 = (bf16[3,3,1280,160]{2,3,1,0:T(8,128)(2,1)S(1)}, bf16[3,3,1280,160]{2,3,1,0:T(8,128)(2,1)}, u32[]{:S(2)}) copy-start(bf16[3,3,1280,160]{2,3,1,0:T(8,128)(2,1)} %param.32) | copy-start | bytes 11059204

commit v3 on v2

--- a/solution.py
+++ b/solution.py
@@ -16,50 +16,73 @@
 both = ("rows", "cols")
 
 
-def call(kernel, out_shape, args, scratch=(), flops=0, outside=(), grant=24):
-    return pl.pallas_call(
+def call(kernel, out_shape, args, scratch=(), flops=0, outside=(), outside_out=(), grant=24):
+    made = pl.pallas_call(
         kernel,
         out_shape=out_shape,
-        in_specs=[pl.BlockSpec(memory_space=pl.ANY if at in outside else pltpu.VMEM) for at in range(len(args))],
-        out_specs=jax.tree.map(lambda _: pl.BlockSpec(memory_space=pltpu.VMEM), out_shape),
+        in_specs=[pl.BlockSpec(memory_space=pltpu.HBM if at in outside else pltpu.VMEM) for at in range(len(args))],
+        out_specs=tuple(
+            pl.BlockSpec(memory_space=pltpu.HBM if at in outside_out else pltpu.VMEM) for at in range(len(out_shape))
+        ),
         scratch_shapes=list(scratch),
         compiler_params=pltpu.CompilerParams(vmem_limit_bytes=grant * 1024 * 1024),
         cost_estimate=pl.CostEstimate(flops=flops, bytes_accessed=0, transcendentals=0),
-    )(*args)
+    )
+    outs = made(*args)
+    return outs if len(outs) > 1 else outs[0]
 
 
 def shape(dims, kind=f32):
     return jax.ShapeDtypeStruct(dims, kind)
 
 
-def exact_dot(left, right):
-    return lax.dot_general(
-        left, right, (((1,), (0,)), ((), ())), precision=lax.Precision.HIGHEST, preferred_element_type=f32
-    )
+def pieces(value):
+    high = value.astype(bf16)
+    rest = value - high.astype(f32)
+    middle = rest.astype(bf16)
+    return high, middle, (rest - middle.astype(f32)).astype(bf16)
+
+
+def joined_rows(first, second):
+    place = lax.broadcasted_iota(jnp.int32, (16, first.shape[1]), 0)
+    found = jnp.zeros((16, first.shape[1]), f32)
+    for at, piece in enumerate(pieces(first) + pieces(second)):
+        found = jnp.where(place == at, piece.astype(f32), found)
+    return found.astype(bf16)
+
+
+def ones_in_group(chan, low, width):
+    return jnp.where((chan >= low) & (chan < low + width), 1.0, 0.0).astype(f32)
 
 
 def to_groups(chans, width, first, lane):
     chan = lax.broadcasted_iota(jnp.int32, (chans, 128), 0) + first
     low = (lax.broadcasted_iota(jnp.int32, (chans, 128), 1) - lane) * width
-    return jnp.where((chan >= low) & (chan < low + width), 1.0, 0.0).astype(f32)
+    return ones_in_group(chan, low, width)
 
 
 def from_groups(chan, width, lane):
     low = (lax.broadcasted_iota(jnp.int32, (128, chan.shape[1]), 0) - lane) * width
-    return jnp.where((chan >= low) & (chan < low + width), 1.0, 0.0).astype(f32)
+    return ones_in_group(chan, low, width)
 
 
 def group_row(sums, squares, width, first, lane):
-    chans = sums.shape[1]
-    row = exact_dot(jnp.broadcast_to(sums, (8, chans)), to_groups(chans, width, first, lane))
-    row += exact_dot(jnp.broadcast_to(squares, (8, chans)), to_groups(chans, width, first, lane + groups))
-    return row[0:1]
+    sums = jnp.sum(sums, axis=0, keepdims=True)
+    squares = jnp.sum(squares, axis=0, keepdims=True)
+    member = to_groups(sums.shape[1], width, first, lane).astype(bf16)
+    found = jnp.dot(joined_rows(sums, squares), member, preferred_element_type=f32)
+    total = found[0:1] + found[1:2] + found[2:3]
+    square = found[3:4] + found[4:5] + found[5:6]
+    return total + pltpu.roll(jnp.broadcast_to(square, (8, 128)), groups, 1)[0:1]
 
 
 def statistics(total, count, width, lane, chan):
-    total = jnp.broadcast_to(total, (8, 128)) / count
-    mean = exact_dot(total, from_groups(chan, width, lane))[0:1]
-    square = exact_dot(total, from_groups(chan, width, lane + groups))[0:1]
+    total = total / count
+    moved = pltpu.roll(jnp.broadcast_to(total, (8, 128)), 128 - groups, 1)[0:1]
+    member = from_groups(chan, width, lane).astype(bf16)
+    found = jnp.dot(joined_rows(total, moved), member, preferred_element_type=f32)
+    mean = found[0:1] + found[1:2] + found[2:3]
+    square = found[3:4] + found[4:5] + found[5:6]
     return mean, lax.rsqrt(square - mean * mean + norm_eps)
 
 
@@ -72,25 +95,52 @@
     return half + half * jnp.tanh(half)
 
 
-def input_sums_kernel(widths, latent_ref, joined_ref, gain_ref, shift_ref, out_ref):
-    def sums_of(ref):
+def start_all(copies):
+    made = [pltpu.make_async_copy(*copy) for copy in copies]
+    for copy in made:
+        copy.start()
+    return made
+
+
+def input_sums_kernel(
+    widths, joined_ref, latent_hbm, gain_hbm, shift_hbm, out_ref, latent_ref, gain_ref, shift_ref, sems
+):
+    half = latent_ref.shape[0] // 2
+    first, second = pl.ds(0, half), pl.ds(half, half)
+    copies = start_all(
+        (
+            (latent_hbm.at[first], latent_ref.at[first], sems.at[0]),
+            (latent_hbm.at[second], latent_ref.at[second], sems.at[1]),
+            (gain_hbm, gain_ref, sems.at[2]),
+            (shift_hbm, shift_ref, sems.at[3]),
+        )
+    )
+
+    def sums_of(ref, begin, end, carry):
         def step(row, carry):
             value = ref[row].astype(f32)
-            return (
-                carry[0] + jnp.sum(value, axis=0, keepdims=True),
-                carry[1] + jnp.sum(value * value, axis=0, keepdims=True),
-            )
-
-        start = jnp.zeros((1, ref.shape[2]), f32)
-        return lax.fori_loop(0, ref.shape[0], step, (start, start))
-
-    row = group_row(*sums_of(latent_ref), widths[0], 0, 0)
-    row += group_row(*sums_of(joined_ref), widths[1], 0, 2 * groups)
+            return carry[0] + folded(value), carry[1] + folded(value * value)
+
+        return lax.fori_loop(begin, end, step, carry, unroll=True)
+
+    def start(ref):
+        zero = jnp.zeros((8, ref.shape[2]), f32)
+        return zero, zero
+
+    three = sums_of(joined_ref, 0, joined_ref.shape[0], start(joined_ref))
+    row = group_row(*three, widths[1], 0, 2 * groups)
+    copies[0].wait()
+    one = sums_of(latent_ref, 0, half, start(latent_ref))
+    copies[1].wait()
+    one = sums_of(latent_ref, half, 2 * half, one)
+    row += group_row(*one, widths[0], 0, 0)
     count = out_ref.shape[0]
     shard = gain_ref.shape[1]
     room = (out_ref.shape[2] - 128) // 2
     out_ref[...] = jnp.zeros_like(out_ref)
     out_ref[:, :, 0:128] = jnp.broadcast_to(row[None], (count, 1, 128))
+    copies[2].wait()
+    copies[3].wait()
     out_ref[:, :, pl.ds(128, shard)] = jnp.broadcast_to(gain_ref[...][None], (count, 1, shard))
     out_ref[:, :, pl.ds(128 + room, shard)] = jnp.broadcast_to(shift_ref[...][None], (count, 1, shard))
 
@@ -115,9 +165,9 @@
     prod_ref[pl.ds(8, blocks * wide), :] = jnp.dot(left, packed_ref[...], preferred_element_type=f32)
 
 
-def shifted_sum(prod_ref, block, wide, keep):
+def shifted_sum(prod_ref, start, keep):
     chans = prod_ref.shape[1] // 3
-    rows = prod_ref[pl.ds(pl.multiple_of(block * wide, 8), wide + 16), :]
+    rows = prod_ref[pl.ds(pl.multiple_of(start, 8), keep + 16), :]
     return (
         rows[7 : 7 + keep, 0:chans]
         + rows[8 : 8 + keep, chans : 2 * chans]
@@ -125,14 +175,18 @@
     )
 
 
+def folded(value):
+    return jnp.sum(value.reshape(value.shape[0] // 8, 8, value.shape[1]), axis=0)
+
+
 def edge_flags(sizes):
     row, col = lax.axis_index("rows"), lax.axis_index("cols")
     return row > 0, row < sizes[0] - 1, col > 0, col < sizes[1] - 1
 
 
 def level_one_first_kernel(
-    count, width, sizes, latent_ref, top_ref, low_ref, side_ref, sums_ref, gain_ref, shift_ref, weight_ref,
-    hid_ref, row_ref, act_ref, packed_ref, prod_ref,
+    count, width, sizes, latent_ref, top_ref, low_ref, side_ref, sums_ref, gain_ref, shift_ref, other_ref, weight_ref,
+    hid_hbm, row_ref, act_ref, packed_ref, prod_ref, hid_ref, hid_sems,
 ):
     rows, cols, chans = latent_ref.shape
     wide = cols + side
@@ -140,7 +194,6 @@
     total = jnp.sum(sums_ref[:, :, 0:128], axis=0)
     mean, inverse = statistics(total, count, width, 0, lane_ids(chans))
     scale, shift = inverse * gain_ref[...], shift_ref[...]
-    pack_level_one(weight_ref, packed_ref)
     place = lax.broadcasted_iota(jnp.int32, (side, chans), 0)
     blocks = rows + 3
 
@@ -161,44 +214,55 @@
         fill(line + 3, latent_ref[line], True, has_right, has_left & ((line < rows - 1) | has_low))
         return carry
 
-    lax.fori_loop(0, rows, main_row, 0)
+    lax.fori_loop(0, rows, main_row, 0, unroll=True)
     fill(rows + 3, low_ref[0], has_low, has_right & has_low, has_left & has_low, blocks)
     fill(rows + 4, low_ref[1], has_low, has_right & has_low, never, blocks)
 
+    pack_level_one(weight_ref, packed_ref)
     products(act_ref, packed_ref, prod_ref)
 
     def combine(block, carry):
-        value = shifted_sum(prod_ref, block, wide, wide)
-        hid_ref[block] = value
-        main = value[0:cols]
         inner = jnp.where((block >= 2) & (block < rows + 2), 1.0, 0.0)
-        main = main * inner
-        return (
-            carry[0] + jnp.sum(main, axis=0, keepdims=True),
-            carry[1] + jnp.sum(main * main, axis=0, keepdims=True),
-        )
-
-    start = jnp.zeros((1, chans), f32)
-    sums, squares = lax.fori_loop(0, blocks, combine, (start, start))
-    row_ref[...] = group_row(sums, squares, width, 0, 0)
+        sums, squares = carry
+        for at in range(0, wide, side):
+            value = shifted_sum(prod_ref, block * wide + at, side)
+            hid_ref[block, pl.ds(at, side), :] = value.astype(bf16)
+            if at < cols:
+                value = value * inner
+                sums, squares = sums + folded(value), squares + folded(value * value)
+        return sums, squares
+
+    start = jnp.zeros((8, chans), f32)
+    carry = (start, start)
+    half = blocks // 2
+    copies = []
+    for at, (begin, end) in enumerate(((0, half), (half, blocks))):
+        carry = lax.fori_loop(begin, end, combine, carry, unroll=True)
+        part = pl.ds(begin, end - begin)
+        copies += start_all(((hid_ref.at[part], hid_hbm.at[part], hid_sems.at[at]),))
+    sums, squares = carry
+    row = other_ref[...] + group_row(sums, squares, width, 0, 0)
+    row_ref[...] = jnp.broadcast_to(row[None], row_ref.shape)
+    for copy in copies:
+        copy.wait()
 
 
 def level_one_second_kernel(
-    count, width, sizes, hid_ref, latent_ref, sums_ref, gain_ref, shift_ref, weight_ref, bias_ref,
+    count, width, sizes, hid_ref, latent_ref, sums_ref, gain_ref, shift_ref, bias_ref, weight_ref,
     out_ref, act_ref, packed_ref, prod_ref,
 ):
+    half = hid_ref.shape[0] // 2
     rows, cols, chans = latent_ref.shape
     wide = cols + side
     has_top, has_low, has_left, has_right = edge_flags(sizes)
     total = jnp.sum(sums_ref[...], axis=0)
     mean, inverse = statistics(total, count, width, 0, lane_ids(chans))
     scale, shift = inverse * gain_ref[...], shift_ref[...]
-    pack_level_one(weight_ref, packed_ref)
     place = lax.broadcasted_iota(jnp.int32, (wide, chans), 0)
     blocks = rows + 1
 
     def fill(block, main_ok, right_ok, left_ok, limit=None):
-        value = activate(hid_ref[block], mean, scale, shift)
+        value = activate(hid_ref[block].astype(f32), mean, scale, shift)
         keep = ((place < cols) & main_ok) | ((place == cols) & right_ok) | ((place == wide - 1) & left_ok)
         store_taps(act_ref, block, jnp.where(keep, value, 0.0).astype(bf16), limit)
 
@@ -210,18 +274,23 @@
         fill(line + 2, True, has_right, has_left & ((line < rows - 1) | has_low))
         return carry
 
-    lax.fori_loop(0, rows - 1, main_row, 0)
+    lax.fori_loop(0, half - 2, main_row, 0, unroll=True)
+    lax.fori_loop(half - 2, rows - 1, main_row, 0, unroll=True)
     fill(rows + 1, True, has_right, has_left & has_low, blocks)
     fill(rows + 2, has_low, has_right & has_low, never, blocks)
 
+    pack_level_one(weight_ref, packed_ref)
     products(act_ref, packed_ref, prod_ref)
 
+
     def combine(line, carry):
-        value = shifted_sum(prod_ref, line + 1, wide, cols)
-        out_ref[line] = (latent_ref[line].astype(f32) + value + bias_ref[...]).astype(bf16)
+        for at in range(0, cols, side):
+            value = shifted_sum(prod_ref, (line + 1) * wide + at, side)
+            cells = pl.ds(at, side)
+            out_ref[line, cells, :] = (latent_ref[line, cells, :].astype(f32) + value + bias_ref[...]).astype(bf16)
         return carry
 
-    lax.fori_loop(0, rows, combine, 0)
+    lax.fori_loop(0, rows, combine, 0, unroll=True)
 
 
 def level_three_taps(left, right):
@@ -240,7 +309,7 @@
 
 
 def level_three_first_kernel(
-    count, width, sizes, near_ref, far_ref, near_edges_ref, far_edges_ref, sums_ref, gain_ref, shift_ref, weight_hbm, other_ref,
+    count, width, sizes, near_ref, far_ref, near_edges_ref, far_edges_ref, sums_ref, gain_ref, shift_ref, weight_hbm,
     hid_ref, local_ref, row_ref, act_ref, raw_ref, prod_ref, weight_ref, weight_sem,
 ):
     chips, height, tile, chans = near_ref.shape
@@ -263,7 +332,7 @@
                 act_ref[line + 1, place, :] = activate(raw.astype(f32), mean, scale, shift).astype(bf16)
                 return carry
 
-            lax.fori_loop(0, height, fill, 0)
+            lax.fori_loop(0, height, fill, 0, unroll=True)
             for at, line, keep in ((0, 0, has_top), (1, lines - 1, has_low)):
                 value = activate(edges[hop, at].astype(f32), mean, scale, shift)
                 act_ref[line, place, :] = jnp.where(keep, value, 0.0).astype(bf16)
@@ -288,11 +357,11 @@
         value = level_three_sum(prod_ref, line, cols, shard)
         hid_ref[line] = value.astype(bf16)
         sums, squares = sums + value, squares + value * value
-    row = other_ref[...]
+    row = jnp.zeros((1, 128), f32)
     for part, lane in ((sums, 2 * groups), (squares, 3 * groups)):
         column = jnp.sum(part, axis=1, keepdims=True)
         row += jnp.sum(column * to_groups(shard, width, col_id * shard, lane), axis=0, keepdims=True)
-    row_ref[...] = jnp.broadcast_to(row[None], row_ref.shape)
+    row_ref[...] = row
 
 
 def level_three_second_kernel(
@@ -363,12 +432,11 @@
     return lax.all_to_all(sent, both, 0, 0)
 
 
-def gathered(own, received, sums):
-    *received, sums = lax.optimization_barrier((*received, sums))
+def gathered(own, received):
     near = jnp.stack([own] + received)
     top, low = neighbours(near[:, 0:1], near[:, -1:], "rows")
     edges = jnp.concatenate([top, low], axis=1)
-    return near, hop_to(near, 1), edges, hop_to(edges, 1), sums
+    return near, hop_to(near, 1), edges, hop_to(edges, 1)
 
 
 def body(
@@ -398,23 +466,18 @@
     room = -(-shard // 128) * 128
     sent = call(
         functools.partial(input_sums_kernel, widths),
-        shape((devices, 1, 128 + 2 * room)),
-        (latent1, joined, row_of(norm3b_g), row_of(norm3b_b)),
+        (shape((devices, 1, 128 + 2 * room)),),
+        (joined, latent1, row_of(norm3b_g), row_of(norm3b_b)),
+        (
+            pltpu.VMEM(latent1.shape, bf16),
+            pltpu.VMEM((1, shard), f32),
+            pltpu.VMEM((1, shard), f32),
+            pltpu.SemaphoreType.DMA((4,)),
+        ),
+        outside=(1, 2, 3),
     )
     sums = exchange(sent)
-    near, far, near_edges, far_edges, sums = gathered(joined, received, sums)
-
-    hid1, row_one = call(
-        functools.partial(level_one_first_kernel, count_one, widths[0], sizes),
-        (shape((rows + 3, wide, chans)), shape((1, 128))),
-        (latent1, top, low, beside, sums, row_of(norm1a_g), row_of(norm1a_b), conv1a_w),
-        (
-            pltpu.VMEM((rows + 3, wide, 3 * chans), bf16),
-            pltpu.VMEM((3 * chans, 3 * chans), bf16),
-            pltpu.VMEM(((rows + 3) * wide + 16, 3 * chans), f32),
-        ),
-        flops=2 * rows * cols * 9 * chans * chans,
-    )
+    near, far, near_edges, far_edges = gathered(joined, received)
 
     flops_three = 2 * height * whole_cols * 9 * deep * shard
     by_input = lambda weight: jnp.swapaxes(weight, 2, 3)
@@ -424,22 +487,38 @@
         pltpu.VMEM((3, 3, shard, deep), bf16),
         pltpu.SemaphoreType.DMA,
     )
-    hid3, local, sent_two = call(
+    hid3, local, row_three = call(
         functools.partial(level_three_first_kernel, count_three, widths[1], sizes),
-        (tile_out, tile_out, shape((devices, 1, 128))),
-        (near, far, near_edges, far_edges, sums, row_of(norm3a_g), row_of(norm3a_b), by_input(conv3a_w), row_one),
+        (tile_out, tile_out, shape((1, 128))),
+        (near, far, near_edges, far_edges, sums, row_of(norm3a_g), row_of(norm3a_b), by_input(conv3a_w)),
         (pltpu.VMEM((height + 2, whole_cols, deep), bf16), pltpu.VMEM((height, whole_cols, deep), bf16)) + three_scratch,
         flops=flops_three,
         outside=(7,),
     )
     received = [hop_to(hid3, 2 * k) for k in range(1, chips)]
+    hid1, sent_two = call(
+        functools.partial(level_one_first_kernel, count_one, widths[0], sizes),
+        (shape((rows + 3, wide, chans), bf16), shape((devices, 1, 128))),
+        (latent1, top, low, beside, sums, row_of(norm1a_g), row_of(norm1a_b), row_three, conv1a_w),
+        (
+            pltpu.VMEM((rows + 3, wide, 3 * chans), bf16),
+            pltpu.VMEM((3 * chans, 3 * chans), bf16),
+            pltpu.VMEM(((rows + 3) * wide + 16, 3 * chans), f32),
+            pltpu.VMEM((rows + 3, wide, chans), bf16),
+            pltpu.SemaphoreType.DMA((2,)),
+        ),
+        flops=2 * rows * cols * 9 * chans * chans,
+        outside_out=(0,),
+    )
+
     sums_two = exchange(sent_two)
-    near_two, far_two, near_edges_two, far_edges_two, sums_two = gathered(hid3, received, sums_two)
+    *received, sums_two = lax.optimization_barrier((*received, sums_two))
+    near_two, far_two, near_edges_two, far_edges_two = gathered(hid3, received)
 
     out1 = call(
         functools.partial(level_one_second_kernel, count_one, widths[0], sizes),
-        shape(latent1.shape, bf16),
-        (hid1, latent1, sums_two, row_of(norm1b_g), row_of(norm1b_b), conv1b_w, row_of(conv1b_b)),
+        (shape(latent1.shape, bf16),),
+        (hid1, latent1, sums_two, row_of(norm1b_g), row_of(norm1b_b), row_of(conv1b_b), conv1b_w),
         (
             pltpu.VMEM((rows + 1, wide, 3 * chans), bf16),
             pltpu.VMEM((3 * chans, 3 * chans), bf16),
@@ -450,7 +529,7 @@
     bias = jnp.pad(row_of(conv3b_b), ((0, 0), (0, room - shard)))
     out3 = call(
         functools.partial(level_three_second_kernel, count_three, widths[1], sizes),
-        tile_out,
+        (tile_out,),
         (near_two, far_two, near_edges_two, far_edges_two, local, sums_two, sums, by_input(conv3b_w), bias),
         (pltpu.VMEM((deep, (height + 2) * whole_cols), bf16),) + three_scratch,
         flops=flops_three,

time: 116 us -> 98.5 us (0.85)
  Pallas kernels: 30 us -> 23.3 us
  blocking collectives: 17.5 us -> 12 us
  waiting for transfers between devices: 21.2 us -> 17 us
  other arithmetic: 3.28 us -> 1.38 us
  starting transfers between devices: 34.4 us -> 36.3 us
    pallas_call x5, Pallas kernels: 30 us -> 23.3 us  [call(): outs = made(*args)]
    all_to_all x1, waiting for transfers between devices: 5.93 us -> 0.01 us  [exchange(): return lax.all_to_all(sent, both, 0, 0)]
    all_to_all x1, blocking collectives: 17.5 us -> 12 us  [exchange(): return lax.all_to_all(sent, both, 0, 0)]
    ppermute x4, starting transfers between devices: 10 us -> 13.8 us  [neighbours(): lax.ppermute(high_edge, axis, forward)]
    unnamed x32 -> x34, local copies, waits for them, and re-layouts: 2.59 us -> 4.61 us
    ppermute x4, waiting for transfers between devices: 1.81 us -> 3.52 us  [neighbours(): lax.ppermute(high_edge, axis, forward)]
    reshape x7, local copies, waits for them, and re-layouts: 1.39 us -> 0.03 us  [body(): row_of = lambda vector: vector.reshape(1, -1)]
  transfers between devices with their start and end apart: 19 -> 19, of which waited for: 5 -> 6; matrix products, arithmetic and copies ran while one was open for 6% -> 2% of each run, Pallas kernels for 17% -> 14%
where the time goes in v3:
time: 98.5 us; the launch traced here: 97.9 us
  starting transfers between devices  36.3 us (37%)
  Pallas kernels  23.3 us (24%)
  waiting for transfers between devices  17 us (17%)
  blocking collectives  12 us (12%)
  local copies, waits for them, and re-layouts  6.69 us (7%)
  other arithmetic  1.38 us (1%)
  between operations  1.28 us (1%)
    pallas_call x5, Pallas kernels, call(): outs = made(*args)  23.3 us
    ppermute x4, starting transfers between devices, neighbours(): lax.ppermute(high_edge, axis, forward)  13.8 us
    ppermute x4, waiting for transfers between devices, neighbours(): lax.ppermute(low_edge, axis, backward)  13.4 us
    all_to_all x1, blocking collectives, exchange(): return lax.all_to_all(sent, both, 0, 0)  12 us
    ppermute x10, starting transfers between devices, hop_to(): lax.ppermute(value, 'cols', [(i, i ^ step) for i in range(lax.axis_size('...  11.1 us
    all_to_all x1, starting transfers between devices, exchange(): return lax.all_to_all(sent, both, 0, 0)  6 us
    ppermute x4, starting transfers between devices, neighbours(): lax.ppermute(low_edge, axis, backward)  5.35 us
    unnamed x34, local copies, waits for them, and re-layouts  4.61 us
  transfers between devices with their start and end apart: 19, of which 6 were waited for; matrix products, arithmetic and copies ran while one was open for 2% of the time, Pallas kernels for 14%

profile of v3, /device:TPU:0, one launch (start us, length us, event | category | flops | bytes accessed | tf_op | source)
XLA Modules:
  0.0 97.9 jit_solution(4131570062996344737)
XLA Ops:
  0.6 1.0 %add_convert_fusion.joined_ref = bf16[4,16,1280]{2,1,0:T(8,128)(2,1)S(1)} fusion(bf16[4,16,1280]{2,1,0:T(8,128)(2,1)} %param.26, bf16[4,16,1280]{2,1,0:T(8,128)(2,1)} %param.25), kind=kLoop, calls=%fused_computation.2 | loop fusion | flops 327680 | bytes 491520 | tf_op jit(solution)/shard_map/convert_element_type | solution.py:460
  1.7 5.1 %collective-permute-start.6 = (bf16[4,16,1280]{2,1,0:T(8,128)(2,1)S(1)}, bf16[4,16,1280]{2,1,0:T(8,128)(2,1)S(1)}, u32[]{:S(2)}, u32[]{:S(2)}) collective-permute-start(bf16[4,16,1280]{2,1,0:T(8,128)(2,1)S(1)} %add_convert_fusion.joined_ref), channel_id=1, source_target_pairs={{0,6},{1,7},{2,4},{3,5},{4,2},{5,3},{6,0},{7,1},{8,14},{9,15},{10,... | collective-permute-start | bytes 491528 | tf_op jit(solution)/shard_map/ppermute | solution.py:428
  6.8 0.0 collective-permute-start.5
  6.8 0.6 collective-permute-start.4
  7.5 1.1 %copy-done = bf16[16,64,320]{2,1,0:T(8,128)(2,1)S(1)} copy-done((bf16[16,64,320]{2,1,0:T(8,128)(2,1)S(1)}, bf16[16,64,320]{2,1,0:T(8,128)(2,1)}, u32[]{:S(2)}) %copy-start) | copy-done | bytes 655384
  8.6 0.7 copy-done.2
  9.3 0.7 copy-done.3
  10.0 1.9 %shard_map.176 = f32[32,1,640]{2,1,0:T(1,128)} custom-call(bf16[4,16,1280]{2,1,0:T(8,128)(2,1)S(1)} %add_convert_fusion.joined_ref, bf16[16,64,320]{2,1,0:T(8,128)(2,1)S(1)} %copy-done, f32[1,160]{1,0:T(1,128)S(1)} %bitcast.16, f32[1,160]{1,0:T(1,128)S(1)} %bitcast.17), custom_call_target="tpu_custom_call" | custom-call | tf_op jit(solution)/shard_map/pallas_call | solution.py:31
  11.9 6.0 %all-to-all-start = ((f32[32,1,640]{2,1,0:T(1,128)}), f32[32,1,640]{2,1,0:T(1,128)S(1)}, u32[]{:S(2)}, u32[]{:S(2)}) async-start(f32[32,1,640]{2,1,0:T(1,128)} %shard_map.176), calls=%async_computation | async-start | bytes 163840 | tf_op jit(solution)/shard_map/all_to_all | solution.py:432
  17.9 1.0 fusion.1
  18.8 1.3 %collective-permute-start.1 = (bf16[2,64,320]{2,1,0:T(8,128)(2,1)S(1)}, bf16[2,64,320]{2,1,0:T(8,128)(2,1)S(1)}, u32[]{:S(2)}, u32[]{:S(2)}) collective-permute-start(bf16[2,64,320]{2,1,0:T(8,128)(2,1)S(1)} %get-tuple-element.22), channel_id=1, source_target_pairs={{8,0},{16,8},{24,16},{9,1},{17,9},{25,17},{10,2},{18,10},{26,18},{... | collective-permute-start | bytes 245768 | tf_op jit(solution)/shard_map/ppermute | solution.py:424
  20.1 4.6 %collective-permute-start = (bf16[2,64,320]{2,1,0:T(8,128)(2,1)S(1)}, bf16[2,64,320]{2,1,0:T(8,128)(2,1)S(1)}, u32[]{:S(2)}, u32[]{:S(2)}) collective-permute-start(bf16[2,64,320]{2,1,0:T(8,128)(2,1)S(1)} %get-tuple-element.23), channel_id=1, source_target_pairs={{0,8},{8,16},{16,24},{1,9},{9,17},{17,25},{2,10},{10,18},{18,26},{... | collective-permute-start | bytes 245768 | tf_op jit(solution)/shard_map/ppermute | solution.py:424
  24.7 1.0 %fusion = (bf16[16,2,320]{2,1,0:T(2,128)(2,1)S(1)}, bf16[16,2,320]{2,1,0:T(2,128)(2,1)S(1)}) fusion(bf16[16,64,320]{2,1,0:T(8,128)(2,1)} %latent_ref.3), kind=kLoop, calls=%fused_computation.10 | loop fusion | bytes 81920 | tf_op jit(solution)/shard_map/slice | solution.py:461
  25.7 0.2 collective-permute-done.1.low_ref
  25.9 0.0 collective-permute-done.6
  25.9 0.0 collective-permute-done.5
  25.9 0.0 collective-permute-done.4
  26.0 0.1 pad_maximum_fusion.near_ref
  26.1 4.4 %collective-permute-start.8 = (bf16[4,1,16,1280]{3,2,1,0:T(8,128)(2,1)S(1)}, bf16[4,1,16,1280]{3,2,1,0:T(8,128)(2,1)S(1)}, u32[]{:S(2)}, u32[]{:S(2)}) collective-permute-start(bf16[4,1,16,1280]{3,2,1,0:T(8,128)(2,1)S(1)} %get-tuple-element.27), channel_id=1, source_target_pairs={{0,8},{8,16},{16,24},{1,9},{9,17},{17,25},{2,10},{10,18},{18,26},{... | collective-permute-start | bytes 491528 | tf_op jit(solution)/shard_map/ppermute | solution.py:424
  30.5 0.0 collective-permute-done.top_ref
  30.5 0.1 collective-permute-start.7
  30.6 1.3 %collective-permute-start.9 = (bf16[4,1,16,1280]{3,2,1,0:T(8,128)(2,1)S(1)}, bf16[4,1,16,1280]{3,2,1,0:T(8,128)(2,1)S(1)}, u32[]{:S(2)}, u32[]{:S(2)}) collective-permute-start(bf16[4,1,16,1280]{3,2,1,0:T(8,128)(2,1)S(1)} %get-tuple-element.26), channel_id=1, source_target_pairs={{8,0},{16,8},{24,16},{9,1},{17,9},{25,17},{10,2},{18,10},{26,18},{... | collective-permute-start | bytes 491528 | tf_op jit(solution)/shard_map/ppermute | solution.py:424
  31.9 1.7 %collective-permute-done.8 = bf16[4,1,16,1280]{3,2,1,0:T(8,128)(2,1)S(1)} collective-permute-done((bf16[4,1,16,1280]{3,2,1,0:T(8,128)(2,1)S(1)}, bf16[4,1,16,1280]{3,2,1,0:T(8,128)(2,1)S(1)}, u32[]{:S(2)}, u32[]{:S(2)}) %collective-permute-start.8) | collective-permute-done | bytes 163872 | tf_op jit(solution)/shard_map/ppermute | solution.py:424
  33.6 5.4 %collective-permute-done.9 = bf16[4,1,16,1280]{3,2,1,0:T(8,128)(2,1)S(1)} collective-permute-done((bf16[4,1,16,1280]{3,2,1,0:T(8,128)(2,1)S(1)}, bf16[4,1,16,1280]{3,2,1,0:T(8,128)(2,1)S(1)}, u32[]{:S(2)}, u32[]{:S(2)}) %collective-permute-start.9) | collective-permute-done | bytes 163872 | tf_op jit(solution)/shard_map/ppermute | solution.py:424
  39.1 0.1 collective-permute-start.10
  39.2 0.1 pad_maximum_fusion.3
  39.2 2.4 %collective-permute-start.3 = (bf16[20,2,320]{2,1,0:T(2,128)(2,1)S(1)}, bf16[20,2,320]{2,1,0:T(2,128)(2,1)S(1)}, u32[]{:S(2)}, u32[]{:S(2)}) collective-permute-start(bf16[20,2,320]{2,1,0:T(2,128)(2,1)S(1)} %pad_maximum_fusion.3), channel_id=1, source_target_pairs={{0,1},{1,2},{2,3},{3,4},{4,5},{5,6},{6,7},{8,9},{9,10},{10,11},{11... | collective-permute-start | bytes 76808 | tf_op jit(solution)/shard_map/ppermute | solution.py:424
  41.6 0.1 pad_maximum_fusion.2
  41.7 1.3 %collective-permute-start.2 = (bf16[20,2,320]{2,1,0:T(2,128)(2,1)S(1)}, bf16[20,2,320]{2,1,0:T(2,128)(2,1)S(1)}, u32[]{:S(2)}, u32[]{:S(2)}) collective-permute-start(bf16[20,2,320]{2,1,0:T(2,128)(2,1)S(1)} %pad_maximum_fusion.2), channel_id=1, source_target_pairs={{1,0},{2,1},{3,2},{4,3},{5,4},{6,5},{7,6},{9,8},{10,9},{11,10},{12... | collective-permute-start | bytes 76808 | tf_op jit(solution)/shard_map/ppermute | solution.py:424
  43.0 0.0 copy-done.8
  43.1 0.0 collective-permute-done.3
  43.1 2.3 %collective-permute-done.2 = bf16[20,2,320]{2,1,0:T(2,128)(2,1)S(1)} collective-permute-done((bf16[20,2,320]{2,1,0:T(2,128)(2,1)S(1)}, bf16[20,2,320]{2,1,0:T(2,128)(2,1)S(1)}, u32[]{:S(2)}, u32[]{:S(2)}) %collective-permute-start.2) | collective-permute-done | bytes 25632 | tf_op jit(solution)/shard_map/ppermute | solution.py:424
  45.4 0.1 pad_add_fusion.side_ref
  45.4 0.0 all-to-all-done.sums_ref.affine_ref
  45.5 0.0 collective-permute-done.10.far_edges_ref
  45.5 0.0 collective-permute-done.7.far_ref
  45.5 0.0 copy-start.4
  45.5 2.0 %copy-done.4 = bf16[3,3,1280,160]{2,3,1,0:T(8,128)(2,1)S(1)} copy-done((bf16[3,3,1280,160]{2,3,1,0:T(8,128)(2,1)S(1)}, bf16[3,3,1280,160]{2,3,1,0:T(8,128)(2,1)}, u32[]{:S(2)}) %copy-start.4) | copy-done | bytes 3686424
  47.5 4.8 %shard_map.177 = (bf16[4,160,128]{2,1,0:T(8,128)(2,1)S(1)}, bf16[4,160,128]{2,1,0:T(8,128)(2,1)S(1)}, f32[1,128]{1,0:T(1,128)S(1)}) custom-call(bf16[4,4,16,1280]{3,2,1,0:T(8,128)(2,1)S(1)} %pad_maximum_fusion.near_ref, bf16[4,4,16,1280]{3,2,1,0:T(8,128)(2,1)S(1)} %collective-permute-done.7.far_ref, ...), custom_call_target="tpu_custom_call" | custom-call | flops 1887436800 | tf_op jit(solution)/shard_map/pallas_call | solution.py:31
  52.3 4.4 %collective-permute-start.13 = (bf16[4,160,128]{2,1,0:T(8,128)(2,1)S(1)}, bf16[4,160,128]{2,1,0:T(8,128)(2,1)S(1)}, u32[]{:S(2)}, u32[]{:S(2)}) collective-permute-start(bf16[4,160,128]{2,1,0:T(8,128)(2,1)S(1)} %get-tuple-element.13), channel_id=1, source_target_pairs={{0,6},{1,7},{2,4},{3,5},{4,2},{5,3},{6,0},{7,1},{8,14},{9,15},{10,... | collective-permute-start | bytes 491528 | tf_op jit(solution)/shard_map/ppermute | solution.py:428
  56.8 0.0 collective-permute-start.12
  56.8 0.6 collective-permute-start.11
  57.4 6.3 %shard_map.178 = (bf16[19,80,320]{2,1,0:T(8,128)(2,1)S(1)}, f32[32,1,128]{2,1,0:T(1,128)S(1)}) custom-call(bf16[16,64,320]{2,1,0:T(8,128)(2,1)S(1)} %copy-done.1, bf16[2,64,320]{2,1,0:T(8,128)(2,1)S(1)} %collective-permute-done.top_ref, bf16[2,64,320]{2,1,0:T(8,128)(2,1)S(1)} %collective-permute-done.1.low_ref, ...), custom_call_target="tpu_custom_call" | custom-call | flops 1887436800 | tf_op jit(solution)/shard_map/pallas_call | solution.py:31
  63.8 0.0 copy-start.12
  63.8 0.0 copy-start.13
  63.8 0.0 copy-start.14
  63.8 0.0 copy-start.15
  63.8 0.0 copy-start.7
  63.8 12.0 %all_to_all.10.sums_ref = f32[32,1,128]{2,1,0:T(1,128)S(1)} all-to-all(f32[32,1,128]{2,1,0:T(1,128)S(1)} %get-tuple-element.14), channel_id=1, replica_groups=mesh['rows'=4,'cols'=8] {'rows','cols'}, dimensions={0} | all-to-all | bytes 32768 | tf_op jit(solution)/shard_map/all_to_all | solution.py:432
  75.8 0.0 collective-permute-done.13
  75.8 0.0 collective-permute-done.12
  75.8 0.0 collective-permute-done.11
  75.8 0.1 pad_maximum_fusion.1.near_ref
  76.0 2.5 %collective-permute-start.15 = (bf16[4,1,160,128]{3,2,1,0:T(8,128)(2,1)S(1)}, bf16[4,1,160,128]{3,2,1,0:T(8,128)(2,1)S(1)}, u32[]{:S(2)}, u32[]{:S(2)}) collective-permute-start(bf16[4,1,160,128]{3,2,1,0:T(8,128)(2,1)S(1)} %get-tuple-element.25), channel_id=1, source_target_pairs={{0,8},{8,16},{16,24},{1,9},{9,17},{17,25},{2,10},{10,18},{18,26},{... | collective-permute-start | bytes 491528 | tf_op jit(solution)/shard_map/ppermute | solution.py:424
  78.5 0.1 collective-permute-start.14
  78.5 1.5 %collective-permute-start.16 = (bf16[4,1,160,128]{3,2,1,0:T(8,128)(2,1)S(1)}, bf16[4,1,160,128]{3,2,1,0:T(8,128)(2,1)S(1)}, u32[]{:S(2)}, u32[]{:S(2)}) collective-permute-start(bf16[4,1,160,128]{3,2,1,0:T(8,128)(2,1)S(1)} %get-tuple-element.24), channel_id=1, source_target_pairs={{8,0},{16,8},{24,16},{9,1},{17,9},{25,17},{10,2},{18,10},{26,18},{... | collective-permute-start | bytes 491528 | tf_op jit(solution)/shard_map/ppermute | solution.py:424
  80.0 1.8 %collective-permute-done.15 = bf16[4,1,160,128]{3,2,1,0:T(8,128)(2,1)S(1)} collective-permute-done((bf16[4,1,160,128]{3,2,1,0:T(8,128)(2,1)S(1)}, bf16[4,1,160,128]{3,2,1,0:T(8,128)(2,1)S(1)}, u32[]{:S(2)}, u32[]{:S(2)}) %collective-permute-start.15) | collective-permute-done | bytes 163872 | tf_op jit(solution)/shard_map/ppermute | solution.py:424
  81.8 5.5 %collective-permute-done.16 = bf16[4,1,160,128]{3,2,1,0:T(8,128)(2,1)S(1)} collective-permute-done((bf16[4,1,160,128]{3,2,1,0:T(8,128)(2,1)S(1)}, bf16[4,1,160,128]{3,2,1,0:T(8,128)(2,1)S(1)}, u32[]{:S(2)}, u32[]{:S(2)}) %collective-permute-start.16) | collective-permute-done | bytes 163872 | tf_op jit(solution)/shard_map/ppermute | solution.py:424
  87.3 0.1 collective-permute-start.17
  87.5 0.0 copy-start.5
  87.5 5.3 %shard_map.179 = bf16[16,64,320]{2,1,0:T(8,128)(2,1)} custom-call(bf16[19,80,320]{2,1,0:T(8,128)(2,1)S(1)} %get-tuple-element.12.hid_ref, bf16[16,64,320]{2,1,0:T(8,128)(2,1)S(1)} %copy-done.1, f32[32,1,128]{2,1,0:T(1,128)S(1)} %all_to_all.10.sums_ref, f32[1,320]{1,0:T(1,128)S(1)} %reshape.40.gain_ref, f32[1,320]{1,0:T(1,128)S(1)} %reshape.41.shift_ref, ...), custom_call_target="tpu_custom_call" | custom-call | flops 1887436800 | tf_op jit(solution)/shard_map/pallas_call | solution.py:31
  92.8 0.0 collective-permute-done.17.far_edges_ref
  92.8 0.0 collective-permute-done.14.far_ref
  92.8 4.9 %shard_map.180 = bf16[4,160,128]{2,1,0:T(8,128)(2,1)} custom-call(bf16[4,4,160,128]{3,2,1,0:T(8,128)(2,1)S(1)} %pad_maximum_fusion.1.near_ref, bf16[4,4,160,128]{3,2,1,0:T(8,128)(2,1)S(1)} %collective-permute-done.14.far_ref, bf16[4,2,160,128]{3,2,1,0:T(8,128)(2,1)S(1)} %constant_dynamic-update-slice_fusion.2.near_edges_ref, ...), custom_call_target="tpu_custom_call" | custom-call | flops 1887436800 | tf_op jit(solution)/shard_map/pallas_call | solution.py:31
  (36 shorter events, 0.2 us)
Async XLA Ops:
  1.7 24.3 %collective-permute-start.6 = (bf16[4,16,1280]{2,1,0:T(8,128)(2,1)S(1)}, bf16[4,16,1280]{2,1,0:T(8,128)(2,1)S(1)}, u32[]{:S(2)}, u32[]{:S(2)}) collective-permute-start(bf16[4,16,1280]{2,1,0:T(8,128)(2,1)S(1)} %add_convert_fusion.joined_ref), channel_id=1, source_target_pairs={{0,6},{1,7},{2,4},{3,5},{4,2},{5,3},{6,0},{7,1},{8,14},{9,15},{10,... | collective-permute-start | bytes 491528 | tf_op jit(solution)/shard_map/ppermute | solution.py:428
  6.8 19.1 %collective-permute-start.5 = (bf16[4,16,1280]{2,1,0:T(8,128)(2,1)S(1)}, bf16[4,16,1280]{2,1,0:T(8,128)(2,1)S(1)}, u32[]{:S(2)}, u32[]{:S(2)}) collective-permute-start(bf16[4,16,1280]{2,1,0:T(8,128)(2,1)S(1)} %add_convert_fusion.joined_ref), channel_id=1, source_target_pairs={{0,4},{1,5},{2,6},{3,7},{4,0},{5,1},{6,2},{7,3},{8,12},{9,13},{10,... | collective-permute-start | bytes 491528 | tf_op jit(solution)/shard_map/ppermute | solution.py:428
  6.8 19.1 %collective-permute-start.4 = (bf16[4,16,1280]{2,1,0:T(8,128)(2,1)S(1)}, bf16[4,16,1280]{2,1,0:T(8,128)(2,1)S(1)}, u32[]{:S(2)}, u32[]{:S(2)}) collective-permute-start(bf16[4,16,1280]{2,1,0:T(8,128)(2,1)S(1)} %add_convert_fusion.joined_ref), channel_id=1, source_target_pairs={{0,2},{1,3},{2,0},{3,1},{4,6},{5,7},{6,4},{7,5},{8,10},{9,11},{10,... | collective-permute-start | bytes 491528 | tf_op jit(solution)/shard_map/ppermute | solution.py:428
  7.5 1.1 %copy-start = (bf16[16,64,320]{2,1,0:T(8,128)(2,1)S(1)}, bf16[16,64,320]{2,1,0:T(8,128)(2,1)}, u32[]{:S(2)}) copy-start(bf16[16,64,320]{2,1,0:T(8,128)(2,1)} %latent_ref.3) | copy-start | bytes 1966084
  8.6 0.7 copy-start.2
  9.3 0.7 copy-start.3
  9.9 33.0 %copy-start.10 = (f32[320]{0:T(512)S(1)}, f32[320]{0:T(512)}, u32[]{:S(2)}) copy-start(f32[320]{0:T(512)} %param.18) | copy-start | bytes 3844
  9.9 33.0 %copy-start.11 = (f32[320]{0:T(512)S(1)}, f32[320]{0:T(512)}, u32[]{:S(2)}) copy-start(f32[320]{0:T(512)} %param.19) | copy-start | bytes 3844
  10.0 33.1 %copy-start.8 = (f32[1280]{0:T(1024)S(1)}, f32[1280]{0:T(1024)}, u32[]{:S(2)}) copy-start(f32[1280]{0:T(1024)} %param.27) | copy-start | bytes 15364
  10.0 33.1 %copy-start.9 = (f32[1280]{0:T(1024)S(1)}, f32[1280]{0:T(1024)}, u32[]{:S(2)}) copy-start(f32[1280]{0:T(1024)} %param.28) | copy-start | bytes 15364
  11.9 33.6 %all-to-all-start = ((f32[32,1,640]{2,1,0:T(1,128)}), f32[32,1,640]{2,1,0:T(1,128)S(1)}, u32[]{:S(2)}, u32[]{:S(2)}) async-start(f32[32,1,640]{2,1,0:T(1,128)} %shard_map.176), calls=%async_computation | async-start | bytes 163840 | tf_op jit(solution)/shard_map/all_to_all | solution.py:432
  18.8 7.1 %collective-permute-start.1 = (bf16[2,64,320]{2,1,0:T(8,128)(2,1)S(1)}, bf16[2,64,320]{2,1,0:T(8,128)(2,1)S(1)}, u32[]{:S(2)}, u32[]{:S(2)}) collective-permute-start(bf16[2,64,320]{2,1,0:T(8,128)(2,1)S(1)} %get-tuple-element.22), channel_id=1, source_target_pairs={{8,0},{16,8},{24,16},{9,1},{17,9},{25,17},{10,2},{18,10},{26,18},{... | collective-permute-start | bytes 245768 | tf_op jit(solution)/shard_map/ppermute | solution.py:424
  20.1 10.3 %collective-permute-start = (bf16[2,64,320]{2,1,0:T(8,128)(2,1)S(1)}, bf16[2,64,320]{2,1,0:T(8,128)(2,1)S(1)}, u32[]{:S(2)}, u32[]{:S(2)}) collective-permute-start(bf16[2,64,320]{2,1,0:T(8,128)(2,1)S(1)} %get-tuple-element.23), channel_id=1, source_target_pairs={{0,8},{8,16},{16,24},{1,9},{9,17},{17,25},{2,10},{10,18},{18,26},{... | collective-permute-start | bytes 245768 | tf_op jit(solution)/shard_map/ppermute | solution.py:424
  26.1 7.5 %collective-permute-start.8 = (bf16[4,1,16,1280]{3,2,1,0:T(8,128)(2,1)S(1)}, bf16[4,1,16,1280]{3,2,1,0:T(8,128)(2,1)S(1)}, u32[]{:S(2)}, u32[]{:S(2)}) collective-permute-start(bf16[4,1,16,1280]{3,2,1,0:T(8,128)(2,1)S(1)} %get-tuple-element.27), channel_id=1, source_target_pairs={{0,8},{8,16},{16,24},{1,9},{9,17},{17,25},{2,10},{10,18},{18,26},{... | collective-permute-start | bytes 491528 | tf_op jit(solution)/shard_map/ppermute | solution.py:424
  30.5 15.0 %collective-permute-start.7 = (bf16[4,4,16,1280]{3,2,1,0:T(8,128)(2,1)S(1)}, bf16[4,4,16,1280]{3,2,1,0:T(8,128)(2,1)S(1)}, u32[]{:S(2)}, u32[]{:S(2)}) collective-permute-start(bf16[4,4,16,1280]{3,2,1,0:T(8,128)(2,1)S(1)} %pad_maximum_fusion.near_ref), channel_id=1, source_target_pairs={{0,1},{1,0},{2,3},{3,2},{4,5},{5,4},{6,7},{7,6},{8,9},{9,8},{10,11... | collective-permute-start | bytes 1966088 | tf_op jit(solution)/shard_map/ppermute | solution.py:428
  30.6 8.5 %collective-permute-start.9 = (bf16[4,1,16,1280]{3,2,1,0:T(8,128)(2,1)S(1)}, bf16[4,1,16,1280]{3,2,1,0:T(8,128)(2,1)S(1)}, u32[]{:S(2)}, u32[]{:S(2)}) collective-permute-start(bf16[4,1,16,1280]{3,2,1,0:T(8,128)(2,1)S(1)} %get-tuple-element.26), channel_id=1, source_target_pairs={{8,0},{16,8},{24,16},{9,1},{17,9},{25,17},{10,2},{18,10},{26,18},{... | collective-permute-start | bytes 491528 | tf_op jit(solution)/shard_map/ppermute | solution.py:424
  39.1 6.4 %collective-permute-start.10 = (bf16[4,2,16,1280]{3,2,1,0:T(8,128)(2,1)S(1)}, bf16[4,2,16,1280]{3,2,1,0:T(8,128)(2,1)S(1)}, u32[]{:S(2)}, u32[]{:S(2)}) collective-permute-start(bf16[4,2,16,1280]{3,2,1,0:T(8,128)(2,1)S(1)} %constant_dynamic-update-slice_fusion.near_edges_ref), channel_id=1, source_target_pairs={{0,1},{1,0},{2,3},{3,2},{4,5},{5,4},{6,7},{7,6},{8,9},{9,8},{10,11... | collective-permute-start | bytes 983048 | tf_op jit(solution)/shard_map/ppermute | solution.py:428
  39.2 3.9 %collective-permute-start.3 = (bf16[20,2,320]{2,1,0:T(2,128)(2,1)S(1)}, bf16[20,2,320]{2,1,0:T(2,128)(2,1)S(1)}, u32[]{:S(2)}, u32[]{:S(2)}) collective-permute-start(bf16[20,2,320]{2,1,0:T(2,128)(2,1)S(1)} %pad_maximum_fusion.3), channel_id=1, source_target_pairs={{0,1},{1,2},{2,3},{3,4},{4,5},{5,6},{6,7},{8,9},{9,10},{10,11},{11... | collective-permute-start | bytes 76808 | tf_op jit(solution)/shard_map/ppermute | solution.py:424
  41.7 3.7 %collective-permute-start.2 = (bf16[20,2,320]{2,1,0:T(2,128)(2,1)S(1)}, bf16[20,2,320]{2,1,0:T(2,128)(2,1)S(1)}, u32[]{:S(2)}, u32[]{:S(2)}) collective-permute-start(bf16[20,2,320]{2,1,0:T(2,128)(2,1)S(1)} %pad_maximum_fusion.2), channel_id=1, source_target_pairs={{1,0},{2,1},{3,2},{4,3},{5,4},{6,5},{7,6},{9,8},{10,9},{11,10},{12... | collective-permute-start | bytes 76808 | tf_op jit(solution)/shard_map/ppermute | solution.py:424
  45.5 2.0 %copy-start.4 = (bf16[3,3,1280,160]{2,3,1,0:T(8,128)(2,1)S(1)}, bf16[3,3,1280,160]{2,3,1,0:T(8,128)(2,1)}, u32[]{:S(2)}) copy-start(bf16[3,3,1280,160]{2,3,1,0:T(8,128)(2,1)} %param.29) | copy-start | bytes 11059204
  47.5 9.9 %copy-start.1 = (bf16[16,64,320]{2,1,0:T(8,128)(2,1)S(1)}, bf16[16,64,320]{2,1,0:T(8,128)(2,1)}, u32[]{:S(2)}) copy-start(bf16[16,64,320]{2,1,0:T(8,128)(2,1)} %latent_ref.3) | copy-start | bytes 1966084
  47.5 9.9 %copy-start.6 = (bf16[3,3,320,320]{3,2,1,0:T(8,128)(2,1)S(1)}, bf16[3,3,320,320]{3,2,1,0:T(8,128)(2,1)}, u32[]{:S(2)}) copy-start(bf16[3,3,320,320]{3,2,1,0:T(8,128)(2,1)} %weight_ref.2) | copy-start | bytes 5529604
  52.3 23.5 %collective-permute-start.13 = (bf16[4,160,128]{2,1,0:T(8,128)(2,1)S(1)}, bf16[4,160,128]{2,1,0:T(8,128)(2,1)S(1)}, u32[]{:S(2)}, u32[]{:S(2)}) collective-permute-start(bf16[4,160,128]{2,1,0:T(8,128)(2,1)S(1)} %get-tuple-element.13), channel_id=1, source_target_pairs={{0,6},{1,7},{2,4},{3,5},{4,2},{5,3},{6,0},{7,1},{8,14},{9,15},{10,... | collective-permute-start | bytes 491528 | tf_op jit(solution)/shard_map/ppermute | solution.py:428
  56.8 19.1 %collective-permute-start.12 = (bf16[4,160,128]{2,1,0:T(8,128)(2,1)S(1)}, bf16[4,160,128]{2,1,0:T(8,128)(2,1)S(1)}, u32[]{:S(2)}, u32[]{:S(2)}) collective-permute-start(bf16[4,160,128]{2,1,0:T(8,128)(2,1)S(1)} %get-tuple-element.13), channel_id=1, source_target_pairs={{0,4},{1,5},{2,6},{3,7},{4,0},{5,1},{6,2},{7,3},{8,12},{9,13},{10,... | collective-permute-start | bytes 491528 | tf_op jit(solution)/shard_map/ppermute | solution.py:428
  56.8 19.1 %collective-permute-start.11 = (bf16[4,160,128]{2,1,0:T(8,128)(2,1)S(1)}, bf16[4,160,128]{2,1,0:T(8,128)(2,1)S(1)}, u32[]{:S(2)}, u32[]{:S(2)}) collective-permute-start(bf16[4,160,128]{2,1,0:T(8,128)(2,1)S(1)} %get-tuple-element.13), channel_id=1, source_target_pairs={{0,2},{1,3},{2,0},{3,1},{4,6},{5,7},{6,4},{7,5},{8,10},{9,11},{10,... | collective-permute-start | bytes 491528 | tf_op jit(solution)/shard_map/ppermute | solution.py:428
  63.8 23.7 %copy-start.12 = (f32[320]{0:T(512)S(1)}, f32[320]{0:T(512)}, u32[]{:S(2)}) copy-start(f32[320]{0:T(512)} %param.21) | copy-start | bytes 3844
  63.8 23.7 %copy-start.13 = (f32[320]{0:T(512)S(1)}, f32[320]{0:T(512)}, u32[]{:S(2)}) copy-start(f32[320]{0:T(512)} %param.22) | copy-start | bytes 3844
  63.8 23.7 %copy-start.14 = (f32[320]{0:T(512)S(1)}, f32[320]{0:T(512)}, u32[]{:S(2)}) copy-start(f32[320]{0:T(512)} %param.24) | copy-start | bytes 3844
  63.8 23.7 %copy-start.15 = (f32[160]{0:T(256)S(1)}, f32[160]{0:T(256)}, u32[]{:S(2)}) copy-start(f32[160]{0:T(256)} %param.33) | copy-start | bytes 1924
  63.8 23.7 %copy-start.7 = (bf16[3,3,320,320]{3,2,1,0:T(8,128)(2,1)S(1)}, bf16[3,3,320,320]{3,2,1,0:T(8,128)(2,1)}, u32[]{:S(2)}) copy-start(bf16[3,3,320,320]{3,2,1,0:T(8,128)(2,1)} %weight_ref.3) | copy-start | bytes 5529604
  76.0 5.8 %collective-permute-start.15 = (bf16[4,1,160,128]{3,2,1,0:T(8,128)(2,1)S(1)}, bf16[4,1,160,128]{3,2,1,0:T(8,128)(2,1)S(1)}, u32[]{:S(2)}, u32[]{:S(2)}) collective-permute-start(bf16[4,1,160,128]{3,2,1,0:T(8,128)(2,1)S(1)} %get-tuple-element.25), channel_id=1, source_target_pairs={{0,8},{8,16},{16,24},{1,9},{9,17},{17,25},{2,10},{10,18},{18,26},{... | collective-permute-start | bytes 491528 | tf_op jit(solution)/shard_map/ppermute | solution.py:424
  78.5 14.3 %collective-permute-start.14 = (bf16[4,4,160,128]{3,2,1,0:T(8,128)(2,1)S(1)}, bf16[4,4,160,128]{3,2,1,0:T(8,128)(2,1)S(1)}, u32[]{:S(2)}, u32[]{:S(2)}) collective-permute-start(bf16[4,4,160,128]{3,2,1,0:T(8,128)(2,1)S(1)} %pad_maximum_fusion.1.near_ref), channel_id=1, source_target_pairs={{0,1},{1,0},{2,3},{3,2},{4,5},{5,4},{6,7},{7,6},{8,9},{9,8},{10,11... | collective-permute-start | bytes 1966088 | tf_op jit(solution)/shard_map/ppermute | solution.py:428
  78.5 8.8 %collective-permute-start.16 = (bf16[4,1,160,128]{3,2,1,0:T(8,128)(2,1)S(1)}, bf16[4,1,160,128]{3,2,1,0:T(8,128)(2,1)S(1)}, u32[]{:S(2)}, u32[]{:S(2)}) collective-permute-start(bf16[4,1,160,128]{3,2,1,0:T(8,128)(2,1)S(1)} %get-tuple-element.24), channel_id=1, source_target_pairs={{8,0},{16,8},{24,16},{9,1},{17,9},{25,17},{10,2},{18,10},{26,18},{... | collective-permute-start | bytes 491528 | tf_op jit(solution)/shard_map/ppermute | solution.py:424
  87.3 5.5 %collective-permute-start.17 = (bf16[4,2,160,128]{3,2,1,0:T(8,128)(2,1)S(1)}, bf16[4,2,160,128]{3,2,1,0:T(8,128)(2,1)S(1)}, u32[]{:S(2)}, u32[]{:S(2)}) collective-permute-start(bf16[4,2,160,128]{3,2,1,0:T(8,128)(2,1)S(1)} %constant_dynamic-update-slice_fusion.2.near_edges_ref), channel_id=1, source_target_pairs={{0,1},{1,0},{2,3},{3,2},{4,5},{5,4},{6,7},{7,6},{8,9},{9,8},{10,11... | collective-permute-start | bytes 983048 | tf_op jit(solution)/shard_map/ppermute | solution.py:428
  87.5 5.3 %copy-start.5 = (bf16[3,3,1280,160]{2,3,1,0:T(8,128)(2,1)S(1)}, bf16[3,3,1280,160]{2,3,1,0:T(8,128)(2,1)}, u32[]{:S(2)}) copy-start(bf16[3,3,1280,160]{2,3,1,0:T(8,128)(2,1)} %param.32) | copy-start | bytes 11059204
